TPU v7x, 256 devices: a whole 4x4x8 slice. The times are simulated.
256 devices in a mesh: branch: 32 (over y, z), tensor: 8 (over x, core).
Axes of the slice: x: 4, y: 4, z: 8, core: 2. Of those that a mesh axis runs over, the one named last changes fastest.
Arguments:
- layer_input: bfloat16 [16384, 5120], P(('branch', 'tensor')), may hold values from -360 to 360
- norm_gain: float32 [5120], replicated, may hold values from 0.25 to 1.75
- projection_weight: bfloat16 [5120, 5120], P(None, 'tensor'), may hold values from -0.078125 to 0.078125
- output_weight: bfloat16 [3072, 5120], P('tensor'), may hold values from -3 to 3
- prompt_cache: bfloat16 [2048, 2048], P(None, 'tensor'), may hold values from -1800 to 1800
- subtree_cache: bfloat16 [2, 16384, 2048], P(None, 'branch', 'tensor'), may hold values from -6 to 6
- parents: int32 [2, 32], replicated, may hold values from 0 to 31
- leaf_scores: float32 [32], P('branch'), may hold values from 0.3 to 1
Outputs:
- attn_output: bfloat16 [16384, 5120], P(('branch', 'tensor'))
- subtree_min: float32 [2, 32], P(None, 'branch')
- subtree_product: float32 [2, 32], P(None, 'branch')
Inputs may be any that keep to these rules, and one draw needn't show every extreme that they name: parents[0, j] is the parent in level one of node j of level two; parents[1, j] is the parent in level two of new node j. Node j of every level is held by branch index j.
All inputs are finite; a program needn't handle non-finite values.
Results may differ from a plain program's by a relative error of at most 0.015.
Values may be sent and summed in bfloat16 or wider, within the bound.
No kernel may reach another device: no remote copies, remote signals or barrier semaphores. Data moves between devices by JAX's collectives and lax.ppermute only.
A program may use at most 128 MiB of HBM per device.

v0:
```python
import jax
import jax.numpy as jnp
from jax import lax
from jax.sharding import PartitionSpec as P

HEAD_SIZE = 128
SEGMENT_TOKENS = 512
PROMPT_TOKENS = 2048


THETA = 1000000.0
EPSILON = 1e-06


def from_everyone(x, axis):
    count = lax.axis_size(axis)
    return lax.all_to_all(jnp.broadcast_to(x[None], (count, *x.shape)), axis, 0, 0, tiled=True)


def all_in_one(x, axis):
    leaves = jax.tree.leaves(x)
    sequence = sorted(range(len(leaves)), key=lambda k: -leaves[k].size)
    width = (1, *leaves[sequence[0]].shape)[-1]
    lines = [
        jnp.pad(leaves[k].reshape(-1), (0, -leaves[k].size % width)).reshape(-1, width)
        for k in sequence
    ]
    both, at, found = (from_everyone(jnp.concatenate(lines), axis), 0, {})
    for k, line in zip(sequence, lines):
        piece = both[:, at : at + len(line)].reshape(len(both), -1)
        found[k] = piece[:, : leaves[k].size].reshape(-1, *leaves[k].shape)
        at += len(line)
    numbers = iter(range(len(leaves)))
    return jax.tree.map(lambda _: found[next(numbers)], x)


def combined_pairwise(pieces, combine):
    while len(jax.tree.leaves(pieces)[0]) > 1:
        pieces = jax.vmap(combine)(
            *(jax.tree.map(lambda part: part[side::2], pieces) for side in (0, 1))
        )
    return jax.tree.map(lambda part: part[0], pieces)


def combined_all(x, axis, combine):
    pieces = all_in_one(x, axis)
    return combined_pairwise(pieces, combine)


def normalize(inputs, gain):
    wide = inputs.astype(jnp.float32)
    scale = lax.rsqrt(jnp.mean(wide * wide, axis=-1, keepdims=True) + EPSILON)
    return (wide * scale * gain).astype(jnp.bfloat16)


def rotate(vectors, offset):
    half = vectors.shape[-1] // 2
    freq = THETA ** (-jnp.arange(half, dtype=jnp.float32) * 2.0 / vectors.shape[-1])
    places = (offset + jnp.arange(vectors.shape[0])).astype(jnp.float32)
    angle = places[:, None] * freq[None, :]
    shape = (vectors.shape[0],) + (1,) * (vectors.ndim - 2) + (half,)
    cosine = jnp.cos(angle).reshape(shape)
    sine = jnp.sin(angle).reshape(shape)
    front = vectors[..., :half]
    back = vectors[..., half:]
    return jnp.concatenate([front * cosine - back * sine, back * cosine + front * sine], -1)


def attend(queries, context):
    keys = context[:, :, 0, :]
    values = context[:, :, 1, :]
    scale = queries.shape[-1] ** (-0.5)
    scores = jnp.einsum("skgd,lkd->kgsl", queries, keys, preferred_element_type=jnp.float32) * scale
    total = context.shape[0]
    count = queries.shape[0]
    key_place = jnp.arange(total)
    query_place = jnp.arange(count) + total - count
    visible = key_place[None, :] <= query_place[:, None]
    scores = jnp.where(visible, scores, -jnp.inf)
    top = jnp.max(scores, axis=-1, keepdims=True)
    expos = jnp.exp(scores - top)
    weights = (expos / jnp.sum(expos, axis=-1, keepdims=True)).astype(jnp.bfloat16)
    mixed = jnp.einsum("kgsl,lkd->skgd", weights, values, preferred_element_type=jnp.float32)
    return mixed.astype(jnp.bfloat16).reshape(count, -1)


def pair_combine(left, right):
    return (jnp.minimum(left[0], right[0]), left[1] * right[1])


def per_device(
    layer_input,
    norm_gain,
    projection_weight,
    output_weight,
    prompt_cache,
    subtree_cache,
    parents,
    leaf_scores,
):
    kv_heads = prompt_cache.shape[1] // (2 * HEAD_SIZE)
    group = projection_weight.shape[1] // (kv_heads * HEAD_SIZE) - 2
    offset = PROMPT_TOKENS + 2 * SEGMENT_TOKENS
    normed = normalize(layer_input, norm_gain)
    packed = jnp.dot(
        lax.all_gather(normed, "tensor", axis=0, tiled=True),
        projection_weight,
        preferred_element_type=jnp.float32,
    )
    packed = packed.reshape(SEGMENT_TOKENS, kv_heads, group + 2, HEAD_SIZE)
    queries = rotate(packed[:, :, :group, :], offset).astype(jnp.bfloat16)
    keys = rotate(packed[:, :, group, :], offset).astype(jnp.bfloat16)
    values = packed[:, :, group + 1, :].astype(jnp.bfloat16)
    own = jnp.stack([keys, values], 2)
    second = parents[1]
    first = parents[0][second]
    position = lax.axis_index("branch")
    held = lax.all_to_all(subtree_cache[None], "branch", split_axis=2, concat_axis=0, tiled=True)
    tree_levels = jnp.arange(2, dtype=jnp.int32)
    picks = jnp.stack([first, second], 1)
    outgoing = held[picks, tree_levels[None, :]]
    arrived = lax.all_to_all(outgoing, "branch", split_axis=0, concat_axis=2, tiled=True)
    blocks = arrived[0]
    blocks = blocks.reshape(2 * SEGMENT_TOKENS, kv_heads, 2, HEAD_SIZE)
    prompt = prompt_cache.reshape(-1, kv_heads, 2, HEAD_SIZE)
    context = jnp.concatenate([prompt, blocks, own], 0)
    mixed = attend(queries, context)
    partial_term = jnp.dot(mixed, output_weight, preferred_element_type=jnp.float32)
    summed = lax.psum_scatter(
        partial_term.astype(jnp.bfloat16).astype(jnp.float32).astype(jnp.bfloat16),
        "tensor",
        scatter_dimension=0,
        tiled=True,
    )
    nodes = jnp.arange(parents.shape[1], dtype=jnp.int32)
    marks = jnp.stack([nodes == first[position], nodes == second[position]], 0)
    filled = jnp.where(marks, leaf_scores[0], 1.0)
    lowest, product = combined_all((filled, filled), "branch", pair_combine)
    subtree_min = lax.dynamic_slice_in_dim(lowest, position, 1, 1)
    subtree_product = lax.dynamic_slice_in_dim(product, position, 1, 1)
    return (summed, subtree_min, subtree_product)


def solution(mesh):
    placed = (
        P(("branch", "tensor"), None),
        P(),
        P(None, "tensor"),
        P("tensor", None),
        P(None, "tensor"),
        P(None, "branch", "tensor"),
        P(),
        P("branch"),
    )
    return jax.shard_map(
        per_device,
        mesh=mesh,
        in_specs=placed,
        out_specs=(P(("branch", "tensor"), None), P(None, "branch"), P(None, "branch")),
        check_vma=False,
    )
```

profile of v0, /device:TPU:8, one launch (start us, length us, event | category | flops | bytes accessed | tf_op | source)
XLA Modules:
  0.0 169.4 jit_solution(4992892851186095734)
XLA Ops:
  7.2 1.3 fusion.4
  8.5 2.2 %fusion.6 = bf16[64,5120]{1,0:T(8,128)(2,1)} fusion(bf16[64,5120]{1,0:T(8,128)(2,1)} %param.8, f32[5120]{0:T(1024)} %param.9, f32[64]{0:T(128)S(1)} %add_rsqrt_fusion), kind=kLoop, calls=%fused_computation.16 | loop fusion | flops 1310720 | bytes 1331456 | tf_op jit(solution)/shard_map/convert_element_type | solution.py:53
  10.7 2.4 %copy.95 = bf16[2,512,256]{2,0,1:T(2,128)(2,1)} copy(bf16[2,512,256]{2,1,0:T(8,128)(2,1)} %param.13) | data formatting | bytes 1048576 | tf_op args[5]
  13.1 11.7 %all-to-all-start = ((bf16[1,2,512,256]{3,1,0,2:T(2,128)(2,1)}), bf16[1,2,512,256]{3,1,0,2:T(2,128)(2,1)S(1)}, u32[]{:S(2)}, u32[]{:S(2)}) async-start(bf16[1,2,512,256]{3,1,0,2:T(2,128)(2,1)} %bitcast.82), calls=%async_computation | async-start | bytes 1048576 | tf_op jit(solution)/shard_map/all_to_all | solution.py:118
  24.8 0.7 fusion.30
  25.5 0.8 fusion.36
  26.3 0.7 gather_fusion
  27.2 1.5 copy.67
  29.4 1.8 %multiply_cosine_fusion = (f32[512,64]{1,0:T(8,128)}, f32[512,64]{1,0:T(8,128)}) fusion(f32[64]{0:T(128)S(1)} %multiply_power_fusion, f32[512]{0:T(512)S(1)} %fusion.29), kind=kLoop, calls=%fused_computation.31 | loop fusion | flops 32768 | bytes 264448 | tf_op jit(solution)/shard_map/cos | solution.py:62
  31.2 9.0 %all-to-all-done = bf16[1,2,512,256]{3,1,0,2:T(2,128)(2,1)S(1)} async-done(((bf16[1,2,512,256]{3,1,0,2:T(2,128)(2,1)}), bf16[1,2,512,256]{3,1,0,2:T(2,128)(2,1)S(1)}, u32[]{:S(2)}, u32[]{:S(2)}) %all-to-all-start) | async-done | bytes 524320 | tf_op jit(solution)/shard_map/all_to_all | solution.py:118
  40.4 1.5 gather_fusion.1
  41.9 7.0 %all-to-all-start.1 = ((bf16[32,2,16,256]{3,2,1,0:T(8,128)(2,1)}), bf16[32,2,16,256]{3,2,1,0:T(8,128)(2,1)S(1)}, u32[]{:S(2)}, u32[]{:S(2)}) async-start(bf16[32,2,16,256]{3,2,1,0:T(8,128)(2,1)} %bitcast.10), calls=%async_computation.1 | async-start | bytes 1048576 | tf_op jit(solution)/shard_map/all_to_all | solution.py:122
  49.1 1.5 iota_compare_fusion
  50.6 13.0 %all-to-all-done.1 = bf16[32,2,16,256]{3,2,1,0:T(8,128)(2,1)S(1)} async-done(((bf16[32,2,16,256]{3,2,1,0:T(8,128)(2,1)}), bf16[32,2,16,256]{3,2,1,0:T(8,128)(2,1)S(1)}, u32[]{:S(2)}, u32[]{:S(2)}) %all-to-all-start.1) | async-done | bytes 524320 | tf_op jit(solution)/shard_map/all_to_all | solution.py:122
  63.7 0.8 copy.72
  64.5 1.2 reshape_squeeze.3
  65.7 0.9 copy.77
  66.6 8.4 %fusion.37 = f32[512,640]{0,1:T(8,128)S(1)} fusion(bf16[512,5120]{1,0:T(8,128)(2,1)} %all-gather.2.cloned.1.call-done, bf16[5120,640]{1,0:T(8,128)(2,1)} %param.10), kind=kOutput, calls=%fused_computation.80 | convolution fusion | flops 3355443200 | bytes 13107200 | tf_op jit(solution)/shard_map/dot_general | solution.py:105
  75.0 0.9 fusion.34
  76.2 1.9 %fusion.25 = (bf16[512,1,1,64]{3,0,2,1:T(8,128)(2,1)}, bf16[512,1,1,64]{3,0,2,1:T(8,128)(2,1)}) fusion(f32[512,1,128]{2,0,1:T(8,128)S(1)} %bitcast.85, f32[64]{0:T(128)S(1)} %multiply_power_fusion, f32[512]{0:T(512)S(1)} %fusion.29), kind=kLoop, calls=%fused_computation.43 | loop fusion | flops 294912 | bytes 395520 | tf_op jit(solution)/shard_map/concatenate | solution.py:66
  78.1 2.2 %copy.91 = f32[512,1,3,64]{3,0,2,1:T(8,128)} copy(f32[512,1,3,64]{0,3,2,1:T(8,128)} %get-tuple-element.5) | data formatting | bytes 786432
  80.3 2.2 %copy.90 = f32[512,1,3,64]{3,0,2,1:T(8,128)} copy(f32[512,1,3,64]{0,3,2,1:T(8,128)} %get-tuple-element.6) | data formatting | bytes 786432
  82.5 2.6 %fusion.11 = (bf16[512,3,64]{2,0,1:T(8,128)(2,1)}, bf16[512,3,64]{2,0,1:T(8,128)(2,1)}) fusion(f32[512,1,3,64]{3,0,2,1:T(8,128)} %copy.91, f32[512,1,3,64]{3,0,2,1:T(8,128)} %copy.90, f32[512,64]{1,0:T(8,128)} %get-tuple-element.12, f32[512,64]{1,0:T(8,128)} %get-tuple-element.11), kind=kLoop, calls=%fused_computation.25 | loop fusion | flops 786432 | bytes 1441792 | tf_op jit(solution)/shard_map/concatenate | solution.py:66
  85.1 2.4 %maximum_maximum_fusion = bf16[3584,1,2,128]{3,0,2,1:T(8,128)(2,1)} fusion(bf16[512,1,1,128]{3,0,2,1:T(8,128)(2,1)S(1)} %copy.89, bf16[512,1,1,64]{3,0,2,1:T(8,128)(2,1)} %get-tuple-element.8, bf16[512,1,1,64]{3,0,2,1:T(8,128)(2,1)} %get-tuple-element.7, bf16[1024,1,2,128]{3,0,2,1:T(8,128)(2,1)S(1)} %copy-done.2, bf16[2048,1,2,128]{3,0,2,1:T(8,128)(2,1)S(1)} %copy.76), kind=kLoop, calls=%fused_computation.11 | loop fusion | flops 9175040 | bytes 3670016 | tf_op jit(solution)/shard_map/concatenate | solution.py:126
  87.5 5.6 %fusion.1 = (f32[3,512]{1,0:T(4,128)S(1)}, f32[3584,512,3]{1,0,2:T(8,128)S(1)}) fusion(pred[512,3584]{0,1:T(8,128)(4,1)S(1)} %iota_compare_fusion, bf16[512,3,64]{2,0,1:T(8,128)(2,1)} %get-tuple-element.4, bf16[512,3,64]{2,0,1:T(8,128)(2,1)} %get-tuple-element.3, bf16[3584,1,2,128]{3,0,2,1:T(8,128)(2,1)} %maximum_maximum_fusion), kind=kOutput, calls=%fused_computation.6 | convolution fusion | flops 1426586112 | bytes 25565184 | tf_op jit(solution)/shard_map/skgd,lkd->kgsl/dot_general | solution.py:73
  93.1 7.3 %copy-done = f32[3584,512,3]{1,0,2:T(8,128)} copy-done((f32[3584,512,3]{1,0,2:T(8,128)}, f32[3584,512,3]{1,0,2:T(8,128)S(1)}, u32[]{:S(2)}) %copy-start) | copy-done | bytes 22020120
  100.4 5.0 %fusion = f32[3,512]{1,0:T(4,128)S(1)} fusion(f32[3584,512,3]{1,0,2:T(8,128)S(1)} %get-tuple-element.17, f32[3,512]{1,0:T(4,128)S(1)} %get-tuple-element.16, pred[512,3584]{0,1:T(8,128)(4,1)S(1)} %iota_compare_fusion), kind=kLoop, calls=%fused_computation.5 | loop fusion | flops 22018560 | bytes 23867392 | tf_op jit(solution)/shard_map/reduce_sum | solution.py:82
  105.5 11.2 %fusion.7 = bf16[128,3,512]{2,0,1:T(8,128)(2,1)S(1)} fusion(f32[3,512]{1,0:T(4,128)S(1)} %fusion, f32[3,512]{1,0:T(4,128)S(1)} %get-tuple-element.16, f32[3584,512,3]{1,0,2:T(8,128)} %copy-done, pred[512,3584]{0,1:T(8,128)(4,1)S(1)} %iota_compare_fusion, bf16[3584,1,2,128]{3,0,2,1:T(8,128)(2,1)} %maximum_maximum_fusion), kind=kOutput, calls=%fused_computation.17 | convolution fusion | flops 1437007872 | bytes 25178112 | tf_op jit(solution)/shard_map/kgsl,lkd->skgd/dot_general | solution.py:83
  116.7 4.7 %convolution_convert_fusion = bf16[512,5120]{1,0:T(8,128)(2,1)} fusion(bf16[512,384]{0,1:T(8,128)(2,1)S(1)} %bitcast.92, bf16[384,5120]{1,0:T(8,128)(2,1)S(1)} %copy-done.1), kind=kOutput, calls=%fused_computation.9 | convolution fusion | flops 2015887360 | bytes 9568256 | tf_op jit(solution)/shard_map/dot_general | solution.py:128
  124.7 15.4 %all_to_all.38 = f32[32,1,128]{2,1,0:T(1,128)S(1)} all-to-all(f32[32,1,128]{2,1,0:T(1,128)S(1)} %reshape.422), channel_id=1, replica_groups=mesh['branch'=32,'tensor'=8] {'branch'}, dimensions={0} | all-to-all | bytes 32768 | tf_op jit(solution)/shard_map/all_to_all | solution.py:17
  141.6 0.7 dynamic-slice_reduce_fusion
  142.4 20.1 %reduce-scatter.2.cloned.1.call-done = bf16[64,5120]{1,0:T(8,128)(2,1)} async-done(((bf16[512,5120]{1,0:T(8,128)(2,1)}), bf16[64,5120]{1,0:T(8,128)(2,1)}) %reduce-scatter.2.cloned.1.call-update) | async-done | bytes 655376 | tf_op jit(solution)/shard_map/reduce_scatter | solution.py:129
  (46 shorter events, 5.6 us)
Async XLA Ops:
  7.2 59.4 %all-gather.2.cloned.1.call-start = ((), (), s32[]{:S(2)}) async-start(), calls=%async_computation.4 | async-start | bytes 5898240 | tf_op jit(solution)/shard_map/all_gather | solution.py:106
  13.1 27.2 %all-to-all-start = ((bf16[1,2,512,256]{3,1,0,2:T(2,128)(2,1)}), bf16[1,2,512,256]{3,1,0,2:T(2,128)(2,1)S(1)}, u32[]{:S(2)}, u32[]{:S(2)}) async-start(bf16[1,2,512,256]{3,1,0,2:T(2,128)(2,1)} %bitcast.82), calls=%async_computation | async-start | bytes 1048576 | tf_op jit(solution)/shard_map/all_to_all | solution.py:118
  41.9 21.8 %all-to-all-start.1 = ((bf16[32,2,16,256]{3,2,1,0:T(8,128)(2,1)}), bf16[32,2,16,256]{3,2,1,0:T(8,128)(2,1)S(1)}, u32[]{:S(2)}, u32[]{:S(2)}) async-start(bf16[32,2,16,256]{3,2,1,0:T(8,128)(2,1)} %bitcast.10), calls=%async_computation.1 | async-start | bytes 1048576 | tf_op jit(solution)/shard_map/all_to_all | solution.py:122
  48.9 113.6 %reduce-scatter.2.cloned.1.call-start = ((), (), s32[]{:S(2)}) async-start(), calls=%async_computation.5 | async-start | bytes 5898240 | tf_op jit(solution)/shard_map/reduce_scatter | solution.py:129
  78.1 7.0 %copy-start.2 = (bf16[1024,1,2,128]{3,0,2,1:T(8,128)(2,1)S(1)}, bf16[1024,1,2,128]{3,0,2,1:T(8,128)(2,1)}, u32[]{:S(2)}) copy-start(bf16[1024,1,2,128]{3,0,2,1:T(8,128)(2,1)} %copy.77) | copy-start | bytes 1572868
  93.1 7.3 %copy-start = (f32[3584,512,3]{1,0,2:T(8,128)}, f32[3584,512,3]{1,0,2:T(8,128)S(1)}, u32[]{:S(2)}) copy-start(f32[3584,512,3]{1,0,2:T(8,128)S(1)} %get-tuple-element.17) | copy-start | bytes 66060292
  105.4 11.2 %copy-start.1 = (bf16[384,5120]{1,0:T(8,128)(2,1)S(1)}, bf16[384,5120]{1,0:T(8,128)(2,1)}, u32[]{:S(2)}) copy-start(bf16[384,5120]{1,0:T(8,128)(2,1)} %param.11) | copy-start | bytes 11796484
Sparse Core Ops, SparseCore 0:
  10.8 41.8 all-gather.1
  121.5 40.9 reduce-scatter.1
where the time goes:
time: 170 us; the launch traced here: 169 us
  waiting for transfers between devices  42.3 us (25%)
  matrix products  30 us (18%)
  local copies, waits for them, and re-layouts  26.2 us (15%)
  other arithmetic  21.5 us (13%)
  starting transfers between devices  19 us (11%)
  blocking collectives  15.4 us (9%)
  between operations  15 us (9%)
    reduce_scatter x1, waiting for transfers between devices, per_device(): lax.psum_scatter(partial_term.astype(jnp.bfloat16).astype(jnp.float32).as...  20.1 us
    unnamed x14, local copies, waits for them, and re-layouts  16.1 us
    all_to_all x1, blocking collectives, from_everyone(): lax.all_to_all(jnp.broadcast_to(x[None], (count, *x.shape)), axis, 0, 0,...  15.4 us
    all_to_all x1, waiting for transfers between devices, per_device(): lax.all_to_all(outgoing, 'branch', split_axis=0, concat_axis=2, tiled=True)  13 us
    all_to_all x1, starting transfers between devices, per_device(): lax.all_to_all(subtree_cache[None], 'branch', split_axis=2, concat_axis=0...  11.7 us
    dot_general x1, matrix products, attend(): jnp.einsum('kgsl,lkd->skgd', weights, values, preferred_element_type=jnp....  11.2 us
    all_to_all x1, waiting for transfers between devices, per_device(): lax.all_to_all(subtree_cache[None], 'branch', split_axis=2, concat_axis=0...  9.03 us
    dot_general x1, matrix products, per_device(): jnp.dot(lax.all_gather(normed, 'tensor', axis=0, tiled=True), projection_...  8.41 us
  transfers between devices with their start and end apart: 4, of which 3 were waited for; matrix products, arithmetic and copies ran while one was open for 11% of the time, Pallas kernels for 0%

commit v1 on v0

v1 whole, which is shorter than its diff:
```python
import functools
import math

import jax
import jax.numpy as jnp
from jax import lax
from jax.experimental import pallas as pl
from jax.experimental.pallas import tpu as pltpu
from jax.sharding import PartitionSpec as P


HEAD_SIZE = 128
SEGMENT_TOKENS = 512
PROMPT_TOKENS = 2048
THETA = 1000000.0
EPSILON = 1e-06

BLOCK = 64
ROWS = 256
DEPTH = 1024
WIDE = 2560
CHUNK = 512

FLOW = [(t, (t + 2) % 8 if t % 2 == 0 else (t - 2) % 8) for t in range(8)]
BACK = [(b, a) for a, b in FLOW]
SWAP = [(t, t ^ 1) for t in range(8)]

VMEM = pl.BlockSpec(memory_space=pltpu.VMEM)
ANY = pl.BlockSpec(memory_space=pl.ANY)
SMEM = pl.BlockSpec(memory_space=pltpu.SMEM)
NT = (((1,), (1,)), ((), ()))
NN = (((1,), (0,)), ((), ()))
TN = (((0,), (0,)), ((), ()))
SCALE = math.log2(math.e) / math.sqrt(HEAD_SIZE)


def matmul(a, b, dims=NN):
    return lax.dot_general(a, b, dims, preferred_element_type=jnp.float32)


def kernel(body, out, mib, flops, scratch=(), specs=None):
    return lambda *args: pl.pallas_call(
        body,
        in_specs=specs or [VMEM] * len(args),
        out_specs=[VMEM] * len(out),
        out_shape=[jax.ShapeDtypeStruct(shape, dtype) for shape, dtype in out],
        scratch_shapes=scratch,
        compiler_params=pltpu.CompilerParams(vmem_limit_bytes=mib << 20),
        cost_estimate=pl.CostEstimate(flops=flops, bytes_accessed=1 << 20, transcendentals=0),
    )(*args)


def slots(member):
    def held(t):
        near_by = lax.rem(t + lax.rem(t, 2) * 4 + 6, 8)
        return near_by, near_by + 1 - 2 * lax.rem(near_by, 2), lax.rem(t + 4, 8)

    partner = member + 1 - 2 * lax.rem(member, 2)
    mine, other = held(member), held(partner)
    return (mine[0], member, other[0], partner), (mine[2], mine[1], other[2], other[1])


def project(group, x0, x1, x2, x3, gain_ref, weight_ref, cos_ref, sin_ref, qkv_ref, scale, total, held, sems):
    steps = x0.shape[1] // DEPTH
    xs = (x0, x1, x2, x3)

    def load(i):
        depth = slice(i * DEPTH, (i + 1) * DEPTH)
        return pltpu.make_async_copy(weight_ref.at[depth, :], held.at[depth, :], sems.at[i])

    for i in range(steps):
        load(i).start()
    for i, x in enumerate(xs):
        wide = x[...].astype(jnp.float32)
        mean = jnp.sum(wide * wide, axis=-1, keepdims=True) * (1.0 / x.shape[1])
        scale[i * BLOCK : (i + 1) * BLOCK, :] = lax.rsqrt(mean + EPSILON)
    for i in range(steps):
        depth = slice(i * DEPTH, (i + 1) * DEPTH)
        gain = gain_ref[:, depth]
        normed = [
            (x[:, depth].astype(jnp.float32) * scale[j * BLOCK : (j + 1) * BLOCK, :] * gain).astype(jnp.bfloat16)
            for j, x in enumerate(xs)
        ]
        load(i).wait()
        term = matmul(jnp.concatenate(normed, 0), held[depth, :])
        total[...] = term if i == 0 else total[...] + term
    blocks = slots(lax.axis_index("tensor"))[group]
    for i in range(4):
        rows = slice(i * BLOCK, (i + 1) * BLOCK)
        cosine = cos_ref[blocks[i]]
        sine = sin_ref[blocks[i]]
        for part in range(4):
            head = total[rows, part * HEAD_SIZE : (part + 1) * HEAD_SIZE]
            turned = head * cosine + pltpu.roll(head, HEAD_SIZE // 2, 1) * sine
            qkv_ref[part, rows, :] = turned.astype(jnp.bfloat16)
        qkv_ref[4, rows, :] = total[rows, 4 * HEAD_SIZE :].astype(jnp.bfloat16)


def extend(state, q, keys, values, mask=None):
    scores = matmul(keys, q, NT) * SCALE
    if mask is not None:
        scores = jnp.where(mask, scores, -jnp.inf)
    top = jnp.max(scores, axis=0, keepdims=True)
    if state is not None:
        top = jnp.maximum(state[0], top)
    expos = jnp.exp2(scores - top)
    total = jnp.sum(expos, axis=0, keepdims=True)
    mixed = matmul(values, expos.astype(jnp.bfloat16), TN)
    if state is not None:
        shrink = jnp.exp2(state[0] - top)
        total = total + state[1] * shrink
        mixed = mixed + state[2] * shrink
    return top, total, mixed


def pick(parents_ref, spread_ref, picked_ref):
    nodes = spread_ref.shape[0]
    older = lax.axis_index("branch") < nodes // 2
    for j in range(nodes):
        second = parents_ref[1, j]
        first = parents_ref[0, second]
        picked_ref[j] = spread_ref[jnp.where(older, first, second)]


def prompt_part(state, q, prompt_ref):
    for c in range(PROMPT_TOKENS // CHUNK):
        rows = slice(c * CHUNK, (c + 1) * CHUNK)
        state = extend(state, q, prompt_ref[rows, :HEAD_SIZE], prompt_ref[rows, HEAD_SIZE:])
    return state


def near_early(qkv_ref, prompt_ref, top_ref, sum_ref, mix_ref):
    q = qkv_ref[:3].reshape(QUERIES, HEAD_SIZE)
    top_ref[...], sum_ref[...], mix_ref[...] = prompt_part(None, q, prompt_ref)


def near_late(prompt_ref, early_ref, te_ref, se_ref, me_ref, late_ref, *results):
    blocks = slots(lax.axis_index("tensor"))
    within = lax.broadcasted_iota(jnp.int32, (BLOCK, QUERIES), 0)
    column = lax.rem(lax.broadcasted_iota(jnp.int32, (1, QUERIES), 1), ROWS)
    for g, qkv_ref in enumerate((early_ref, late_ref)):
        q = qkv_ref[:3].reshape(QUERIES, HEAD_SIZE)
        state = (te_ref[...], se_ref[...], me_ref[...]) if g == 0 else prompt_part(None, q, prompt_ref)
        place = jnp.zeros((1, QUERIES), jnp.int32)
        for i in range(4):
            place = jnp.where(column // BLOCK == i, blocks[g][i] * BLOCK + column - i * BLOCK, place)
        for h, own_ref in enumerate((early_ref, late_ref)):
            mask = jnp.concatenate([within + blocks[h][i] * BLOCK <= place for i in range(4)], 0)
            state = extend(state, q, own_ref[3], own_ref[4], mask)
        for ref, value in zip(results[3 * g : 3 * g + 3], state):
            ref[...] = value


def far(qkv_ref, context_ref, top_ref, sum_ref, mix_ref, mine_ref, other_ref):
    q = qkv_ref[:3].reshape(QUERIES, HEAD_SIZE)
    parts = []
    for columns in (slice(0, QUERIES // 2), slice(QUERIES // 2, QUERIES)):
        state = (top_ref[:, columns], sum_ref[:, columns], mix_ref[:, columns])
        state = extend(state, q[columns], context_ref[:, :HEAD_SIZE], context_ref[:, HEAD_SIZE:])
        parts.append((state[2] / state[1]).T.astype(jnp.bfloat16))
    mixed = jnp.concatenate(parts, 0)
    for head in range(3):
        columns = slice(head * HEAD_SIZE, (head + 1) * HEAD_SIZE)
        mine_ref[:, columns] = mixed[head * ROWS : head * ROWS + ROWS // 2]
        other_ref[:, columns] = mixed[head * ROWS + ROWS // 2 : (head + 1) * ROWS]


def output(a_ref, b_ref, wa_ref, wb_ref, *refs):
    first_ref, second_ref, held, sems = refs[-4:]
    depth = wa_ref.shape[0]
    copies = []
    for c in range(wa_ref.shape[1] // WIDE):
        columns = slice(c * WIDE, (c + 1) * WIDE)
        copies.append(pltpu.make_async_copy(wa_ref.at[:, columns], held.at[:depth, columns], sems.at[2 * c]))
        copies.append(pltpu.make_async_copy(wb_ref.at[:, columns], held.at[depth:, columns], sems.at[2 * c + 1]))
    for copy in copies:
        copy.start()
    both = jnp.concatenate([a_ref[...], b_ref[...]], 1)
    for c in range(wa_ref.shape[1] // WIDE):
        columns = slice(c * WIDE, (c + 1) * WIDE)
        copies[2 * c].wait()
        copies[2 * c + 1].wait()
        total = matmul(both, held[:, columns])
        first = total[:BLOCK]
        if len(refs) > 4:
            first = first + refs[0][:, columns].astype(jnp.float32)
        first_ref[:, columns] = first.astype(jnp.bfloat16)
        second_ref[:, columns] = total[BLOCK:].astype(jnp.bfloat16)


QUERIES = 3 * ROWS
PROJECT_MIB, OUTPUT_MIB = 50, 53
F32, BF16 = jnp.float32, jnp.bfloat16
STATE = [((1, QUERIES), F32), ((1, QUERIES), F32), ((HEAD_SIZE, QUERIES), F32)]


def add(*terms):
    return sum(term.astype(jnp.float32) for term in terms).astype(jnp.bfloat16)


def tables():
    half = HEAD_SIZE // 2
    freq = THETA ** (-jnp.arange(half, dtype=jnp.float32) * 2.0 / HEAD_SIZE)
    places = (PROMPT_TOKENS + 2 * SEGMENT_TOKENS + jnp.arange(SEGMENT_TOKENS)).astype(jnp.float32)
    angle = places[:, None] * freq[None, :]
    cosine, sine = jnp.cos(angle), jnp.sin(angle)
    shape = (SEGMENT_TOKENS // BLOCK, BLOCK, HEAD_SIZE)
    return (
        jnp.concatenate([cosine, cosine], -1).reshape(shape),
        jnp.concatenate([-sine, sine], -1).reshape(shape),
    )


def per_device(
    layer_input, norm_gain, projection_weight, output_weight, prompt_cache, subtree_cache, parents, leaf_scores
):
    position = lax.axis_index("branch")
    nodes = lax.axis_size("branch")
    features = layer_input.shape[1]

    def tensor(x, pairs):
        return lax.ppermute(x, "tensor", pairs)

    x0 = layer_input
    x1 = tensor(x0, SWAP)
    x2 = tensor(x0, FLOW)
    x3 = tensor(x1, FLOW)
    x4 = tensor(x2, FLOW)
    x5 = tensor(x2, SWAP)
    x6 = tensor(x3, SWAP)
    x7 = tensor(x4, SWAP)

    pieces = subtree_cache.reshape(nodes, -1, subtree_cache.shape[2])
    spread = lax.all_to_all(pieces, "branch", 0, 0, tiled=True)

    cosine, sine = tables()
    gain = norm_gain[None, :]
    projected = [((5, ROWS, HEAD_SIZE), BF16)]
    columns = projection_weight.shape[1]
    run_project = lambda group, *xs: kernel(
        functools.partial(project, group),
        projected,
        PROJECT_MIB,
        2 * ROWS * features * columns,
        [
            pltpu.VMEM((ROWS, 1), F32),
            pltpu.VMEM((ROWS, columns), F32),
            pltpu.VMEM((features, columns), BF16),
            pltpu.SemaphoreType.DMA((features // DEPTH,)),
        ],
        [VMEM] * 5 + [ANY] + [VMEM] * 2,
    )(*xs, gain, projection_weight, cosine, sine)
    early = run_project(0, x2, x0, x5, x1)
    early_state = kernel(near_early, STATE, 16, 4 * QUERIES * PROMPT_TOKENS * HEAD_SIZE)(*early, prompt_cache)

    spread, early_state = lax.optimization_barrier((spread, early_state))
    picked = kernel(pick, [(spread.shape, BF16)], 16, 1 << 22, (), [SMEM, VMEM])(parents, spread)[0]
    context = lax.all_to_all(picked, "branch", 0, 0, tiled=True)
    context = context.reshape(2 * SEGMENT_TOKENS, -1)
    other_weight = tensor(lax.optimization_barrier((output_weight, early_state))[0], SWAP)

    late = run_project(1, x4, x3, x7, x6)
    depth = output_weight.shape[0]
    state = kernel(near_late, STATE + STATE, 20, 4 * QUERIES * (PROMPT_TOKENS + 2 * SEGMENT_TOKENS) * HEAD_SIZE)(
        prompt_cache, *early, *early_state, *late
    )

    scores = jnp.broadcast_to(leaf_scores[:, None], (1, HEAD_SIZE))
    for bit in range(5):
        if bit == 1:
            scores, state = lax.optimization_barrier((scores, state))
        came = lax.ppermute(scores, "branch", [(b, b ^ (1 << bit)) for b in range(32)])
        upper = (position >> bit) & 1 == 1
        scores = jnp.where(upper, jnp.concatenate([came, scores]), jnp.concatenate([scores, came]))
    scores = scores[:, 0]

    halves = [((ROWS // 2, 3 * HEAD_SIZE), BF16)] * 2
    run_far = kernel(far, halves, 16, 4 * QUERIES * 2 * SEGMENT_TOKENS * HEAD_SIZE)
    rows = [((BLOCK, features), BF16)] * 2
    run_output = lambda *args: kernel(
        output,
        rows,
        OUTPUT_MIB,
        8 * BLOCK * depth * features,
        [pltpu.VMEM((2 * depth, features), BF16), pltpu.SemaphoreType.DMA((2 * features // WIDE,))],
        [VMEM, VMEM, ANY, ANY, VMEM][: len(args)],
    )(*args)
    late_mine, late_other = run_far(late[0], context, *state[3:])
    late_came = tensor(late_other, SWAP)
    early_mine, early_other = run_far(early[0], context, *state[:3])
    early_came = tensor(early_other, SWAP)
    y4, y3 = run_output(late_mine, late_came, output_weight, other_weight)
    z2 = tensor(y4, BACK)
    z1 = tensor(y3, BACK)
    y2, y0 = run_output(early_mine, early_came, output_weight, other_weight, z2)
    z0 = tensor(y2, BACK)
    z1 = tensor(z1, SWAP)
    attn_output = add(y0, z0, z1)

    second = parents[1]
    owners = jnp.stack([parents[0][second], second])
    filled = jnp.where(owners == position, scores[None, :], 1.0)
    subtree_min = jnp.min(filled, axis=1, keepdims=True)
    subtree_product = jnp.prod(filled, axis=1, keepdims=True)
    return attn_output, subtree_min, subtree_product


def solution(mesh):
    placed = (
        P(("branch", "tensor"), None),
        P(),
        P(None, "tensor"),
        P("tensor", None),
        P(None, "tensor"),
        P(None, "branch", "tensor"),
        P(),
        P("branch"),
    )
    return jax.shard_map(
        per_device,
        mesh=mesh,
        in_specs=placed,
        out_specs=(P(("branch", "tensor"), None), P(None, "branch"), P(None, "branch")),
        check_vma=False,
    )
```

time: 170 us -> 107 us (0.63)
  Pallas kernels: 0 us -> 32.7 us
  matrix products: 30 us -> 0 us
  local copies, waits for them, and re-layouts: 26.2 us -> 4.76 us
  starting transfers between devices: 19 us -> 36.5 us
  other arithmetic: 21.5 us -> 4.22 us
  waiting for transfers between devices: 42.3 us -> 25.4 us
  blocking collectives: 15.4 us -> 0 us
  between operations: 15 us -> 1.55 us
    pallas_call x0 -> x9, Pallas kernels: none -> 32.7 us  [kernel(): pl.pallas_call(body, in_specs=specs or [VMEM] * len(args), out_specs=[VME...]
    dot_general x4 -> x0, matrix products: 30 us -> none  [the longest x1 11.2 us: attend(): jnp.einsum('kgsl,lkd->skgd', weights, values, preferred_element_type=jnp....]
    ppermute x0 -> x19, waiting for transfers between devices: none -> 20.7 us  [the longest x14 12.4 us: tensor(): return lax.ppermute(x, 'tensor', pairs)]
    reduce_scatter x1 -> x0, waiting for transfers between devices: 20.1 us -> none  [per_device(): lax.psum_scatter(partial_term.astype(jnp.bfloat16).astype(jnp.float32).as...]
    ppermute x0 -> x19, starting transfers between devices: none -> 17.5 us  [the longest x5 11 us: per_device(): lax.ppermute(scores, 'branch', [(b, b ^ 1 << bit) for b in range(32)])]
    all_to_all x2, waiting for transfers between devices: 22.1 us -> 4.68 us  [the longest x1 4.68 us: per_device(): spread = lax.all_to_all(pieces, 'branch', 0, 0, tiled=True)]
    all_to_all x1 -> x0, blocking collectives: 15.4 us -> none  [from_everyone(): lax.all_to_all(jnp.broadcast_to(x[None], (count, *x.shape)), axis, 0, 0,...]
    unnamed x14 -> x26, local copies, waits for them, and re-layouts: 16.1 us -> 4.06 us
  transfers between devices with their start and end apart: 4 -> 21, of which waited for: 3 -> 10; matrix products, arithmetic and copies ran while one was open for 11% -> 3% of each run, Pallas kernels for 0% -> 27%
where the time goes in v1:
time: 107 us; the launch traced here: 105 us
  starting transfers between devices  36.5 us (34%)
  Pallas kernels  32.7 us (31%)
  waiting for transfers between devices  25.4 us (24%)
  local copies, waits for them, and re-layouts  4.76 us (4%)
  other arithmetic  4.22 us (4%)
  between operations  1.55 us (1%)
    pallas_call x9, Pallas kernels, kernel(): pl.pallas_call(body, in_specs=specs or [VMEM] * len(args), out_specs=[VME...  32.7 us
    ppermute x14, waiting for transfers between devices, tensor(): return lax.ppermute(x, 'tensor', pairs)  12.4 us
    all_to_all x1, starting transfers between devices, per_device(): spread = lax.all_to_all(pieces, 'branch', 0, 0, tiled=True)  11.7 us
    ppermute x5, starting transfers between devices, per_device(): lax.ppermute(scores, 'branch', [(b, b ^ 1 << bit) for b in range(32)])  11 us
    ppermute x5, waiting for transfers between devices, per_device(): lax.ppermute(scores, 'branch', [(b, b ^ 1 << bit) for b in range(32)])  8.33 us
    all_to_all x1, starting transfers between devices, per_device(): context = lax.all_to_all(picked, 'branch', 0, 0, tiled=True)  7.29 us
    ppermute x14, starting transfers between devices, tensor(): return lax.ppermute(x, 'tensor', pairs)  6.46 us
    all_to_all x1, waiting for transfers between devices, per_device(): spread = lax.all_to_all(pieces, 'branch', 0, 0, tiled=True)  4.68 us
  transfers between devices with their start and end apart: 21, of which 10 were waited for; matrix products, arithmetic and copies ran while one was open for 3% of the time, Pallas kernels for 27%

profile of v1, /device:TPU:8, one launch (start us, length us, event | category | flops | bytes accessed | tf_op | source)
XLA Modules:
  0.0 105.1 jit_solution(4692588866598283782)
XLA Ops:
  0.6 1.6 %collective-permute-start = (bf16[64,5120]{1,0:T(8,128)(2,1)}, bf16[64,5120]{1,0:T(8,128)(2,1)S(1)}, u32[]{:S(2)}, u32[]{:S(2)}) collective-permute-start(bf16[64,5120]{1,0:T(8,128)(2,1)} %x1.1), channel_id=1, source_target_pairs={{0,2},{1,7},{2,4},{3,1},{4,6},{5,3},{6,0},{7,5},{8,10},{9,15},{10,... | collective-permute-start | bytes 1966088 | tf_op jit(solution)/shard_map/ppermute | solution.py:222
  2.2 11.7 %all-to-all-start = ((bf16[32,32,256]{2,1,0:T(8,128)(2,1)}), bf16[32,32,256]{2,1,0:T(8,128)(2,1)S(1)}, u32[]{:S(2)}, u32[]{:S(2)}) async-start(bf16[32,32,256]{2,1,0:T(8,128)(2,1)} %bitcast.19), calls=%async_computation | async-start | bytes 1048576 | tf_op jit(solution)/shard_map/all_to_all | solution.py:234
  14.6 1.0 fusion
  16.3 0.9 collective-permute-done.1.x2
  17.3 4.4 %shard_map.103.qkv_ref.early_ref = bf16[5,256,128]{2,1,0:T(8,128)(2,1)S(1)} custom-call(bf16[64,5120]{1,0:T(8,128)(2,1)S(1)} %collective-permute-done.x0, bf16[64,5120]{1,0:T(8,128)(2,1)S(1)} %copy-done, bf16[64,5120]{1,0:T(8,128)(2,1)S(1)} %collective-permute-done.1.x2, bf16[64,5120]{1,0:T(8,128)(2,1)S(1)} %collective-permute-done.2.x3, ...), custom_call_target="tpu_custom_call" | custom-call | flops 1677721600 | bytes 1048576 | tf_op jit(solution)/shard_map/pallas_call | solution.py:42
  21.7 2.6 %shard_map.104 = (f32[1,768]{1,0:T(1,128)S(1)}, f32[1,768]{1,0:T(1,128)S(1)}, f32[128,768]{1,0:T(8,128)S(1)}) custom-call(bf16[5,256,128]{2,1,0:T(8,128)(2,1)S(1)} %shard_map.103.qkv_ref.early_ref, bf16[2048,256]{1,0:T(8,128)(2,1)S(1)} %copy-done.8), custom_call_target="tpu_custom_call" | custom-call | flops 805306368 | bytes 1048576 | tf_op jit(solution)/shard_map/pallas_call | solution.py:42
  25.8 4.7 %all-to-all-done.spread_ref = bf16[32,32,256]{2,1,0:T(8,128)(2,1)S(1)} async-done(((bf16[32,32,256]{2,1,0:T(8,128)(2,1)}), bf16[32,32,256]{2,1,0:T(8,128)(2,1)S(1)}, u32[]{:S(2)}, u32[]{:S(2)}) %all-to-all-start) | async-done | bytes 524320 | tf_op jit(solution)/shard_map/all_to_all | solution.py:234
  31.1 1.4 %shard_map.105 = bf16[32,32,256]{2,1,0:T(8,128)(2,1)} custom-call(s32[2,32]{1,0:T(2,128)S(1)} %copy-done.7, bf16[32,32,256]{2,1,0:T(8,128)(2,1)S(1)} %all-to-all-done.spread_ref), custom_call_target="tpu_custom_call" | custom-call | flops 4194304 | bytes 1048576 | tf_op jit(solution)/shard_map/pallas_call | solution.py:42
  32.5 7.3 %all-to-all-start.1 = ((bf16[32,32,256]{2,1,0:T(8,128)(2,1)}), bf16[32,32,256]{2,1,0:T(8,128)(2,1)S(1)}, u32[]{:S(2)}, u32[]{:S(2)}) async-start(bf16[32,32,256]{2,1,0:T(8,128)(2,1)} %shard_map.105), calls=%async_computation.1 | async-start | bytes 1048576 | tf_op jit(solution)/shard_map/all_to_all | solution.py:258
  39.8 2.5 %collective-permute-done.4.x0 = bf16[64,5120]{1,0:T(8,128)(2,1)S(1)} collective-permute-done((bf16[64,5120]{1,0:T(8,128)(2,1)S(1)}, bf16[64,5120]{1,0:T(8,128)(2,1)S(1)}, u32[]{:S(2)}, u32[]{:S(2)}) %collective-permute-start.4) | collective-permute-done | bytes 655392 | tf_op jit(solution)/shard_map/ppermute | solution.py:222
  42.3 7.1 %collective-permute-done.5.x1 = bf16[64,5120]{1,0:T(8,128)(2,1)} collective-permute-done((bf16[64,5120]{1,0:T(8,128)(2,1)S(1)}, bf16[64,5120]{1,0:T(8,128)(2,1)}, u32[]{:S(2)}, u32[]{:S(2)}) %collective-permute-start.5) | collective-permute-done | bytes 655392 | tf_op jit(solution)/shard_map/ppermute | solution.py:222
  50.1 2.5 %collective-permute-start.3 = (f32[1,128]{1,0:T(1,128)S(1)}, f32[1,128]{1,0:T(1,128)S(1)}, u32[]{:S(2)}, u32[]{:S(2)}) collective-permute-start(f32[1,128]{1,0:T(1,128)S(1)} %broadcast_in_dim.36), channel_id=1, source_target_pairs={{0,8},{8,0},{16,24},{24,16},{32,40},{40,32},{48,56},{56,48},{64,72... | collective-permute-start | bytes 1544 | tf_op jit(solution)/shard_map/ppermute | solution.py:272
  52.6 1.5 %collective-permute-done.3 = f32[1,128]{1,0:T(1,128)S(1)} collective-permute-done((f32[1,128]{1,0:T(1,128)S(1)}, f32[1,128]{1,0:T(1,128)S(1)}, u32[]{:S(2)}, u32[]{:S(2)}) %collective-permute-start.3) | collective-permute-done | bytes 544 | tf_op jit(solution)/shard_map/ppermute | solution.py:272
  54.2 0.8 copy-done.6
  55.0 5.5 %shard_map.106.late_ref.qkv_ref = bf16[5,256,128]{2,1,0:T(8,128)(2,1)S(1)} custom-call(bf16[64,5120]{1,0:T(8,128)(2,1)S(1)} %collective-permute-done.4.x0, bf16[64,5120]{1,0:T(8,128)(2,1)} %collective-permute-done.5.x1, bf16[64,5120]{1,0:T(8,128)(2,1)S(1)} %collective-permute-done.6.x2, bf16[64,5120]{1,0:T(8,128)(2,1)S(1)} %collective-permute-done.7.x3, ...), custom_call_target="tpu_custom_call" | custom-call | flops 1677721600 | bytes 1048576 | tf_op jit(solution)/shard_map/pallas_call | solution.py:42
  60.6 4.4 %shard_map.107 = (f32[1,768]{1,0:T(1,128)S(1)}, f32[1,768]{1,0:T(1,128)S(1)}, f32[128,768]{1,0:T(8,128)S(1)}, f32[1,768]{1,0:T(1,128)S(1)}, f32[1,768]{1,0:T(1,128)S(1)}, /*index=5*/f32[128,768]{1,0:T(8,128)S(1)}) custom-call(bf16[2048,256]{1,0:T(8,128)(2,1)S(1)} %copy-done.9, bf16[5,256,128]{2,1,0:T(8,128)(2,1)S(1)} %copy-done.2, ...), custom_call_target="tpu_custom_call" | custom-call | flops 1207959552 | bytes 1048576 | tf_op jit(solution)/shard_map/pallas_call | solution.py:42
  65.0 1.0 copy-done.4
  66.0 1.8 %shard_map.109 = (bf16[128,384]{1,0:T(8,128)(2,1)S(1)}, bf16[128,384]{1,0:T(8,128)(2,1)S(1)}) custom-call(bf16[5,256,128]{2,1,0:T(8,128)(2,1)S(1)} %copy-done.4, bf16[1024,256]{1,0:T(8,128)(2,1)S(1)} %bitcast.15, f32[1,768]{1,0:T(1,128)S(1)} %get-tuple-element.51.top_ref, f32[1,768]{1,0:T(1,128)S(1)} %get-tuple-element.52.sum_ref, ...), custom_call_target="tpu_custom_call" | custom-call | flops 402653184 | bytes 1048576 | tf_op jit(solution)/shard_map/pallas_call | solution.py:42
  67.8 1.3 %collective-permute-done.10.b_ref = bf16[128,384]{1,0:T(8,128)(2,1)S(1)} collective-permute-done((bf16[128,384]{1,0:T(8,128)(2,1)S(1)}, bf16[128,384]{1,0:T(8,128)(2,1)S(1)}, u32[]{:S(2)}, u32[]{:S(2)}) %collective-permute-start.10) | collective-permute-done | bytes 98336 | tf_op jit(solution)/shard_map/ppermute | solution.py:222
  69.1 4.9 %shard_map.110 = (bf16[64,5120]{1,0:T(8,128)(2,1)S(1)}, bf16[64,5120]{1,0:T(8,128)(2,1)}) custom-call(bf16[128,384]{1,0:T(8,128)(2,1)S(1)} %get-tuple-element.54.a_ref, bf16[128,384]{1,0:T(8,128)(2,1)S(1)} %collective-permute-done.10.b_ref, bf16[384,5120]{1,0:T(8,128)(2,1)} %wa_ref.3, bf16[384,5120]{1,0:T(8,128)(2,1)} %collective-permute-done.9.wb_ref), custom_call_target="tpu_custom_call" | custom-call | flops 1006632960 | bytes 1048576 | tf_op jit(solution)/shard_map/pallas_call | solution.py:42
  74.6 1.8 %collective-permute-start.13 = (bf16[64,5120]{1,0:T(8,128)(2,1)}, bf16[64,5120]{1,0:T(8,128)(2,1)}, u32[]{:S(2)}, u32[]{:S(2)}) collective-permute-start(bf16[64,5120]{1,0:T(8,128)(2,1)} %get-tuple-element.59), channel_id=1, source_target_pairs={{2,0},{7,1},{4,2},{1,3},{6,4},{3,5},{0,6},{5,7},{10,8},{15,9},{12,... | collective-permute-start | bytes 1966088 | tf_op jit(solution)/shard_map/ppermute | solution.py:222
  76.9 1.8 %shard_map.108 = (bf16[128,384]{1,0:T(8,128)(2,1)S(1)}, bf16[128,384]{1,0:T(8,128)(2,1)S(1)}) custom-call(bf16[5,256,128]{2,1,0:T(8,128)(2,1)S(1)} %copy-done.2, bf16[1024,256]{1,0:T(8,128)(2,1)S(1)} %bitcast.16, f32[1,768]{1,0:T(1,128)S(1)} %get-tuple-element.45.top_ref, f32[1,768]{1,0:T(1,128)S(1)} %get-tuple-element.46.sum_ref, ...), custom_call_target="tpu_custom_call" | custom-call | flops 402653184 | bytes 1048576 | tf_op jit(solution)/shard_map/pallas_call | solution.py:42
  78.7 2.2 %collective-permute-done.15 = f32[2,128]{1,0:T(2,128)S(1)} collective-permute-done((f32[2,128]{1,0:T(2,128)S(1)}, f32[2,128]{1,0:T(2,128)S(1)}, u32[]{:S(2)}, u32[]{:S(2)}) %collective-permute-start.15) | collective-permute-done | bytes 1056 | tf_op jit(solution)/shard_map/ppermute | solution.py:272
  80.9 4.5 %collective-permute-start.16 = (f32[4,128]{1,0:T(4,128)S(1)}, f32[4,128]{1,0:T(4,128)S(1)}, u32[]{:S(2)}, u32[]{:S(2)}) collective-permute-start(f32[4,128]{1,0:T(4,128)S(1)} %maximum_select_fusion.2), channel_id=1, source_target_pairs={{0,32},{8,40},{16,48},{24,56},{32,0},{40,8},{48,16},{56,24},{64,96... | collective-permute-start | bytes 6152 | tf_op jit(solution)/shard_map/ppermute | solution.py:272
  85.4 0.8 copy-done.12
  86.3 6.0 %shard_map.111 = (bf16[64,5120]{1,0:T(8,128)(2,1)S(1)}, bf16[64,5120]{1,0:T(8,128)(2,1)}) custom-call(bf16[128,384]{1,0:T(8,128)(2,1)S(1)} %get-tuple-element.48.a_ref, bf16[128,384]{1,0:T(8,128)(2,1)S(1)} %collective-permute-done.8.b_ref, bf16[384,5120]{1,0:T(8,128)(2,1)} %wa_ref.3, bf16[384,5120]{1,0:T(8,128)(2,1)} %collective-permute-done.9.wb_ref, ...), custom_call_target="tpu_custom_call" | custom-call | flops 1006632960 | bytes 1048576 | tf_op jit(solution)/shard_map/pallas_call | solution.py:42
  92.2 1.1 %collective-permute-start.12 = (bf16[64,5120]{1,0:T(8,128)(2,1)S(1)}, bf16[64,5120]{1,0:T(8,128)(2,1)S(1)}, u32[]{:S(2)}, u32[]{:S(2)}) collective-permute-start(bf16[64,5120]{1,0:T(8,128)(2,1)S(1)} %get-tuple-element.58), channel_id=1, source_target_pairs={{2,0},{7,1},{4,2},{1,3},{6,4},{3,5},{0,6},{5,7},{10,8},{15,9},{12,... | collective-permute-start | bytes 1966088 | tf_op jit(solution)/shard_map/ppermute | solution.py:222
  93.3 1.5 %collective-permute-start.17 = (f32[8,128]{1,0:T(8,128)S(1)}, f32[8,128]{1,0:T(8,128)S(1)}, u32[]{:S(2)}, u32[]{:S(2)}) collective-permute-start(f32[8,128]{1,0:T(8,128)S(1)} %maximum_select_fusion.1), channel_id=1, source_target_pairs={{0,64},{8,72},{16,80},{24,88},{32,96},{40,104},{48,112},{56,120},{... | collective-permute-start | bytes 12296 | tf_op jit(solution)/shard_map/ppermute | solution.py:272
  94.8 2.2 %collective-permute-done.17 = f32[8,128]{1,0:T(8,128)S(1)} collective-permute-done((f32[8,128]{1,0:T(8,128)S(1)}, f32[8,128]{1,0:T(8,128)S(1)}, u32[]{:S(2)}, u32[]{:S(2)}) %collective-permute-start.17) | collective-permute-done | bytes 4128 | tf_op jit(solution)/shard_map/ppermute | solution.py:272
  97.0 2.0 %collective-permute-start.18 = (f32[16,128]{1,0:T(8,128)S(1)}, f32[16,128]{1,0:T(8,128)S(1)}, u32[]{:S(2)}, u32[]{:S(2)}) collective-permute-start(f32[16,128]{1,0:T(8,128)S(1)} %maximum_select_fusion), channel_id=1, source_target_pairs={{0,128},{8,136},{16,144},{24,152},{32,160},{40,168},{48,176},{56,1... | collective-permute-start | bytes 24584 | tf_op jit(solution)/shard_map/ppermute | solution.py:272
  99.7 2.5 %collective-permute-done.18 = f32[16,128]{1,0:T(8,128)S(1)} collective-permute-done((f32[16,128]{1,0:T(8,128)S(1)}, f32[16,128]{1,0:T(8,128)S(1)}, u32[]{:S(2)}, u32[]{:S(2)}) %collective-permute-start.18) | collective-permute-done | bytes 8224 | tf_op jit(solution)/shard_map/ppermute | solution.py:272
  103.0 2.2 %add_convert_fusion = bf16[64,5120]{1,0:T(8,128)(2,1)} fusion(bf16[64,5120]{1,0:T(8,128)(2,1)S(1)} %collective-permute-done.14, bf16[64,5120]{1,0:T(8,128)(2,1)S(1)} %collective-permute-done.12, bf16[64,5120]{1,0:T(8,128)(2,1)} %get-tuple-element.57), kind=kLoop, calls=%fused_computation.1 | loop fusion | flops 1966080 | bytes 2621440 | tf_op jit(solution)/shard_map/convert_element_type | solution.py:198
  (61 shorter events, 6.3 us)
Async XLA Ops:
  0.6 13.7 %collective-permute-start = (bf16[64,5120]{1,0:T(8,128)(2,1)}, bf16[64,5120]{1,0:T(8,128)(2,1)S(1)}, u32[]{:S(2)}, u32[]{:S(2)}) collective-permute-start(bf16[64,5120]{1,0:T(8,128)(2,1)} %x1.1), channel_id=1, source_target_pairs={{0,2},{1,7},{2,4},{3,1},{4,6},{5,3},{6,0},{7,5},{8,10},{9,15},{10,... | collective-permute-start | bytes 1966088 | tf_op jit(solution)/shard_map/ppermute | solution.py:222
  2.2 28.3 %all-to-all-start = ((bf16[32,32,256]{2,1,0:T(8,128)(2,1)}), bf16[32,32,256]{2,1,0:T(8,128)(2,1)S(1)}, u32[]{:S(2)}, u32[]{:S(2)}) async-start(bf16[32,32,256]{2,1,0:T(8,128)(2,1)} %bitcast.19), calls=%async_computation | async-start | bytes 1048576 | tf_op jit(solution)/shard_map/all_to_all | solution.py:234
  13.9 3.4 %copy-start = (bf16[64,5120]{1,0:T(8,128)(2,1)S(1)}, bf16[64,5120]{1,0:T(8,128)(2,1)}, u32[]{:S(2)}) copy-start(bf16[64,5120]{1,0:T(8,128)(2,1)} %x1.1) | copy-start | bytes 1966084
  13.9 3.4 %copy-start.5 = (f32[5120]{0:T(1024)S(1)}, f32[5120]{0:T(1024)}, u32[]{:S(2)}) copy-start(f32[5120]{0:T(1024)} %param.9) | copy-start | bytes 61444
  13.9 2.4 %collective-permute-start.2 = (bf16[64,5120]{1,0:T(8,128)(2,1)}, bf16[64,5120]{1,0:T(8,128)(2,1)S(1)}, u32[]{:S(2)}, u32[]{:S(2)}) collective-permute-start(bf16[64,5120]{1,0:T(8,128)(2,1)} %x1.1), channel_id=1, source_target_pairs={{0,1},{1,0},{2,3},{3,2},{4,5},{5,4},{6,7},{7,6},{8,9},{9,8},{10,11... | collective-permute-start | bytes 1966088 | tf_op jit(solution)/shard_map/ppermute | solution.py:222
  14.3 3.0 %collective-permute-start.1 = (bf16[64,5120]{1,0:T(8,128)(2,1)S(1)}, bf16[64,5120]{1,0:T(8,128)(2,1)S(1)}, u32[]{:S(2)}, u32[]{:S(2)}) collective-permute-start(bf16[64,5120]{1,0:T(8,128)(2,1)S(1)} %collective-permute-done.x0), channel_id=1, source_target_pairs={{0,1},{1,0},{2,3},{3,2},{4,5},{5,4},{6,7},{7,6},{8,9},{9,8},{10,11... | collective-permute-start | bytes 1966088 | tf_op jit(solution)/shard_map/ppermute | solution.py:222
  17.3 4.5 %copy-start.8 = (bf16[2048,256]{1,0:T(8,128)(2,1)S(1)}, bf16[2048,256]{1,0:T(8,128)(2,1)}, u32[]{:S(2)}) copy-start(bf16[2048,256]{1,0:T(8,128)(2,1)} %prompt_ref.3) | copy-start | bytes 3145732
  21.7 9.4 %copy-start.7 = (s32[2,32]{1,0:T(2,128)S(1)}, s32[2,32]{1,0:T(2,128)}, u32[]{:S(2)}) copy-start(s32[2,32]{1,0:T(2,128)} %parents_ref.1) | copy-start | bytes 772
  30.5 38.6 %collective-permute-start.9 = (bf16[384,5120]{1,0:T(8,128)(2,1)}, bf16[384,5120]{1,0:T(8,128)(2,1)}, u32[]{:S(2)}, u32[]{:S(2)}) collective-permute-start(bf16[384,5120]{1,0:T(8,128)(2,1)} %wa_ref.3), channel_id=1, source_target_pairs={{0,1},{1,0},{2,3},{3,2},{4,5},{5,4},{6,7},{7,6},{8,9},{9,8},{10,11... | collective-permute-start | bytes 11796488 | tf_op jit(solution)/shard_map/ppermute | solution.py:222
  30.5 11.8 %collective-permute-start.4 = (bf16[64,5120]{1,0:T(8,128)(2,1)S(1)}, bf16[64,5120]{1,0:T(8,128)(2,1)S(1)}, u32[]{:S(2)}, u32[]{:S(2)}) collective-permute-start(bf16[64,5120]{1,0:T(8,128)(2,1)S(1)} %collective-permute-done.x0), channel_id=1, source_target_pairs={{0,2},{1,7},{2,4},{3,1},{4,6},{5,3},{6,0},{7,5},{8,10},{9,15},{10,... | collective-permute-start | bytes 1966088 | tf_op jit(solution)/shard_map/ppermute | solution.py:222
  30.5 18.9 %collective-permute-start.5 = (bf16[64,5120]{1,0:T(8,128)(2,1)S(1)}, bf16[64,5120]{1,0:T(8,128)(2,1)}, u32[]{:S(2)}, u32[]{:S(2)}) collective-permute-start(bf16[64,5120]{1,0:T(8,128)(2,1)S(1)} %collective-permute-done.2.x3), channel_id=1, source_target_pairs={{0,2},{1,7},{2,4},{3,1},{4,6},{5,3},{6,0},{7,5},{8,10},{9,15},{10,... | collective-permute-start | bytes 1966088 | tf_op jit(solution)/shard_map/ppermute | solution.py:222
  32.5 32.4 %all-to-all-start.1 = ((bf16[32,32,256]{2,1,0:T(8,128)(2,1)}), bf16[32,32,256]{2,1,0:T(8,128)(2,1)S(1)}, u32[]{:S(2)}, u32[]{:S(2)}) async-start(bf16[32,32,256]{2,1,0:T(8,128)(2,1)} %shard_map.105), calls=%async_computation.1 | async-start | bytes 1048576 | tf_op jit(solution)/shard_map/all_to_all | solution.py:258
  42.3 11.9 %collective-permute-start.6 = (bf16[64,5120]{1,0:T(8,128)(2,1)S(1)}, bf16[64,5120]{1,0:T(8,128)(2,1)S(1)}, u32[]{:S(2)}, u32[]{:S(2)}) collective-permute-start(bf16[64,5120]{1,0:T(8,128)(2,1)S(1)} %collective-permute-done.4.x0), channel_id=1, source_target_pairs={{0,1},{1,0},{2,3},{3,2},{4,5},{5,4},{6,7},{7,6},{8,9},{9,8},{10,11... | collective-permute-start | bytes 1966088 | tf_op jit(solution)/shard_map/ppermute | solution.py:222
  49.4 4.8 %collective-permute-start.7 = (bf16[64,5120]{1,0:T(8,128)(2,1)}, bf16[64,5120]{1,0:T(8,128)(2,1)S(1)}, u32[]{:S(2)}, u32[]{:S(2)}) collective-permute-start(bf16[64,5120]{1,0:T(8,128)(2,1)} %collective-permute-done.5.x1), channel_id=1, source_target_pairs={{0,1},{1,0},{2,3},{3,2},{4,5},{5,4},{6,7},{7,6},{8,9},{9,8},{10,11... | collective-permute-start | bytes 1966088 | tf_op jit(solution)/shard_map/ppermute | solution.py:222
  50.1 4.1 %collective-permute-start.3 = (f32[1,128]{1,0:T(1,128)S(1)}, f32[1,128]{1,0:T(1,128)S(1)}, u32[]{:S(2)}, u32[]{:S(2)}) collective-permute-start(f32[1,128]{1,0:T(1,128)S(1)} %broadcast_in_dim.36), channel_id=1, source_target_pairs={{0,8},{8,0},{16,24},{24,16},{32,40},{40,32},{48,56},{56,48},{64,72... | collective-permute-start | bytes 1544 | tf_op jit(solution)/shard_map/ppermute | solution.py:272
  54.2 6.4 %copy-start.2 = (bf16[5,256,128]{2,1,0:T(8,128)(2,1)S(1)}, bf16[5,256,128]{2,1,0:T(8,128)(2,1)}, u32[]{:S(2)}) copy-start(bf16[5,256,128]{2,1,0:T(8,128)(2,1)} %copy-done.1) | copy-start | bytes 983044
  54.2 0.8 copy-start.6
  55.0 5.6 %copy-start.9 = (bf16[2048,256]{1,0:T(8,128)(2,1)S(1)}, bf16[2048,256]{1,0:T(8,128)(2,1)}, u32[]{:S(2)}) copy-start(bf16[2048,256]{1,0:T(8,128)(2,1)} %prompt_ref.3) | copy-start | bytes 3145732
  55.0 5.6 %copy-start.11 = (f32[128,768]{1,0:T(8,128)S(1)}, f32[128,768]{1,0:T(8,128)}, u32[]{:S(2)}) copy-start(f32[128,768]{1,0:T(8,128)} %copy-done.10) | copy-start | bytes 1179652
  60.6 4.4 %copy-start.3 = (bf16[5,256,128]{2,1,0:T(8,128)(2,1)}, bf16[5,256,128]{2,1,0:T(8,128)(2,1)S(1)}, u32[]{:S(2)}) copy-start(bf16[5,256,128]{2,1,0:T(8,128)(2,1)S(1)} %shard_map.106.late_ref.qkv_ref) | copy-start | bytes 983044
  65.0 1.0 copy-start.4
  67.7 1.4 %collective-permute-start.10 = (bf16[128,384]{1,0:T(8,128)(2,1)S(1)}, bf16[128,384]{1,0:T(8,128)(2,1)S(1)}, u32[]{:S(2)}, u32[]{:S(2)}) collective-permute-start(bf16[128,384]{1,0:T(8,128)(2,1)S(1)} %get-tuple-element.55), channel_id=1, source_target_pairs={{0,1},{1,0},{2,3},{3,2},{4,5},{5,4},{6,7},{7,6},{8,9},{9,8},{10,11... | collective-permute-start | bytes 294920 | tf_op jit(solution)/shard_map/ppermute | solution.py:222
  74.0 11.4 %collective-permute-start.11 = (bf16[64,5120]{1,0:T(8,128)(2,1)S(1)}, bf16[64,5120]{1,0:T(8,128)(2,1)S(1)}, u32[]{:S(2)}, u32[]{:S(2)}) collective-permute-start(bf16[64,5120]{1,0:T(8,128)(2,1)S(1)} %get-tuple-element.56), channel_id=1, source_target_pairs={{2,0},{7,1},{4,2},{1,3},{6,4},{3,5},{0,6},{5,7},{10,8},{15,9},{12,... | collective-permute-start | bytes 1966088 | tf_op jit(solution)/shard_map/ppermute | solution.py:222
  74.6 18.7 %collective-permute-start.13 = (bf16[64,5120]{1,0:T(8,128)(2,1)}, bf16[64,5120]{1,0:T(8,128)(2,1)}, u32[]{:S(2)}, u32[]{:S(2)}) collective-permute-start(bf16[64,5120]{1,0:T(8,128)(2,1)} %get-tuple-element.59), channel_id=1, source_target_pairs={{2,0},{7,1},{4,2},{1,3},{6,4},{3,5},{0,6},{5,7},{10,8},{15,9},{12,... | collective-permute-start | bytes 1966088 | tf_op jit(solution)/shard_map/ppermute | solution.py:222
  76.4 4.5 %collective-permute-start.15 = (f32[2,128]{1,0:T(2,128)S(1)}, f32[2,128]{1,0:T(2,128)S(1)}, u32[]{:S(2)}, u32[]{:S(2)}) collective-permute-start(f32[2,128]{1,0:T(2,128)S(1)} %pad_select_fusion), channel_id=1, source_target_pairs={{0,16},{8,24},{16,0},{24,8},{32,48},{40,56},{48,32},{56,40},{64,80... | collective-permute-start | bytes 3080 | tf_op jit(solution)/shard_map/ppermute | solution.py:272
  78.6 6.8 %collective-permute-start.8 = (bf16[128,384]{1,0:T(8,128)(2,1)S(1)}, bf16[128,384]{1,0:T(8,128)(2,1)S(1)}, u32[]{:S(2)}, u32[]{:S(2)}) collective-permute-start(bf16[128,384]{1,0:T(8,128)(2,1)S(1)} %get-tuple-element.49), channel_id=1, source_target_pairs={{0,1},{1,0},{2,3},{3,2},{4,5},{5,4},{6,7},{7,6},{8,9},{9,8},{10,11... | collective-permute-start | bytes 294920 | tf_op jit(solution)/shard_map/ppermute | solution.py:222
  80.9 12.4 %collective-permute-start.16 = (f32[4,128]{1,0:T(4,128)S(1)}, f32[4,128]{1,0:T(4,128)S(1)}, u32[]{:S(2)}, u32[]{:S(2)}) collective-permute-start(f32[4,128]{1,0:T(4,128)S(1)} %maximum_select_fusion.2), channel_id=1, source_target_pairs={{0,32},{8,40},{16,48},{24,56},{32,0},{40,8},{48,16},{56,24},{64,96... | collective-permute-start | bytes 6152 | tf_op jit(solution)/shard_map/ppermute | solution.py:272
  85.4 0.8 copy-start.12
  92.2 10.7 %collective-permute-start.12 = (bf16[64,5120]{1,0:T(8,128)(2,1)S(1)}, bf16[64,5120]{1,0:T(8,128)(2,1)S(1)}, u32[]{:S(2)}, u32[]{:S(2)}) collective-permute-start(bf16[64,5120]{1,0:T(8,128)(2,1)S(1)} %get-tuple-element.58), channel_id=1, source_target_pairs={{2,0},{7,1},{4,2},{1,3},{6,4},{3,5},{0,6},{5,7},{10,8},{15,9},{12,... | collective-permute-start | bytes 1966088 | tf_op jit(solution)/shard_map/ppermute | solution.py:222
  93.3 9.7 %collective-permute-start.14 = (bf16[64,5120]{1,0:T(8,128)(2,1)}, bf16[64,5120]{1,0:T(8,128)(2,1)S(1)}, u32[]{:S(2)}, u32[]{:S(2)}) collective-permute-start(bf16[64,5120]{1,0:T(8,128)(2,1)} %collective-permute-done.13), channel_id=1, source_target_pairs={{0,1},{1,0},{2,3},{3,2},{4,5},{5,4},{6,7},{7,6},{8,9},{9,8},{10,11... | collective-permute-start | bytes 1966088 | tf_op jit(solution)/shard_map/ppermute | solution.py:222
  93.3 3.7 %collective-permute-start.17 = (f32[8,128]{1,0:T(8,128)S(1)}, f32[8,128]{1,0:T(8,128)S(1)}, u32[]{:S(2)}, u32[]{:S(2)}) collective-permute-start(f32[8,128]{1,0:T(8,128)S(1)} %maximum_select_fusion.1), channel_id=1, source_target_pairs={{0,64},{8,72},{16,80},{24,88},{32,96},{40,104},{48,112},{56,120},{... | collective-permute-start | bytes 12296 | tf_op jit(solution)/shard_map/ppermute | solution.py:272
  97.0 5.2 %collective-permute-start.18 = (f32[16,128]{1,0:T(8,128)S(1)}, f32[16,128]{1,0:T(8,128)S(1)}, u32[]{:S(2)}, u32[]{:S(2)}) collective-permute-start(f32[16,128]{1,0:T(8,128)S(1)} %maximum_select_fusion), channel_id=1, source_target_pairs={{0,128},{8,136},{16,144},{24,152},{32,160},{40,168},{48,176},{56,1... | collective-permute-start | bytes 24584 | tf_op jit(solution)/shard_map/ppermute | solution.py:272
  (2 other events, 1.5 us)

commit v2 on v1

--- a/solution.py
+++ b/solution.py
@@ -19,6 +19,7 @@
 ROWS = 256
 DEPTH = 1024
 WIDE = 2560
+SPARE = 8
 CHUNK = 512
 
 FLOW = [(t, (t + 2) % 8 if t % 2 == 0 else (t - 2) % 8) for t in range(8)]
@@ -113,13 +114,43 @@
     return top, total, mixed
 
 
-def pick(parents_ref, spread_ref, picked_ref):
-    nodes = spread_ref.shape[0]
+def pick(parents_ref, score_ref, spread_ref, picked_ref):
+    nodes, rows, _ = spread_ref.shape
     older = lax.axis_index("branch") < nodes // 2
+    score = jnp.full((SPARE, HEAD_SIZE), score_ref[0], jnp.float32)
+    high = score.astype(jnp.bfloat16).astype(jnp.float32)
+    middle = (score - high).astype(jnp.bfloat16).astype(jnp.float32)
+    low = score - high - middle
+    row = lax.broadcasted_iota(jnp.int32, score.shape, 0)
+    terms = jnp.where(row == 0, high, jnp.where(row == 1, middle, low)).astype(jnp.bfloat16)
     for j in range(nodes):
         second = parents_ref[1, j]
-        first = parents_ref[0, second]
-        picked_ref[j] = spread_ref[jnp.where(older, first, second)]
+        source = jnp.where(older, parents_ref[0, second], second)
+        picked_ref[j, :rows] = spread_ref[source, :, :HEAD_SIZE]
+        picked_ref[j, rows : 2 * rows] = spread_ref[source, :, HEAD_SIZE:]
+        picked_ref[j, 2 * rows :] = terms
+
+
+def tree(parents_ref, context_ref, min_ref, product_ref):
+    nodes = context_ref.shape[0]
+    me = lax.axis_index("branch")
+    terms = context_ref[:, -SPARE:, :].astype(jnp.float32)
+    scores = (terms[:, 0, :] + terms[:, 1, :]) + terms[:, 2, :]
+    for level in range(2):
+        least = product = jnp.ones((1, HEAD_SIZE), jnp.float32)
+        for j in range(nodes):
+            second = parents_ref[1, j]
+            owner = parents_ref[0, second] if level == 0 else second
+            term = jnp.where(owner == me, scores[j : j + 1], 1.0)
+            least = jnp.minimum(least, term)
+            product = product * term
+        min_ref[level : level + 1, :] = least[:, :1]
+        product_ref[level : level + 1, :] = product[:, :1]
+
+
+def join(*refs):
+    total = sum(ref[...].astype(jnp.float32) for ref in refs[:-1])
+    refs[-1][...] = total.astype(refs[-1].dtype)
 
 
 def prompt_part(state, q, prompt_ref):
@@ -153,10 +184,13 @@
 
 def far(qkv_ref, context_ref, top_ref, sum_ref, mix_ref, mine_ref, other_ref):
     q = qkv_ref[:3].reshape(QUERIES, HEAD_SIZE)
+    rows = (context_ref.shape[1] - SPARE) // 2
+    keys = context_ref[:, :rows, :].reshape(-1, HEAD_SIZE)
+    values = context_ref[:, rows : 2 * rows, :].reshape(-1, HEAD_SIZE)
     parts = []
     for columns in (slice(0, QUERIES // 2), slice(QUERIES // 2, QUERIES)):
         state = (top_ref[:, columns], sum_ref[:, columns], mix_ref[:, columns])
-        state = extend(state, q[columns], context_ref[:, :HEAD_SIZE], context_ref[:, HEAD_SIZE:])
+        state = extend(state, q[columns], keys, values)
         parts.append((state[2] / state[1]).T.astype(jnp.bfloat16))
     mixed = jnp.concatenate(parts, 0)
     for head in range(3):
@@ -165,8 +199,7 @@
         other_ref[:, columns] = mixed[head * ROWS + ROWS // 2 : (head + 1) * ROWS]
 
 
-def output(a_ref, b_ref, wa_ref, wb_ref, *refs):
-    first_ref, second_ref, held, sems = refs[-4:]
+def output(a_ref, b_ref, wa_ref, wb_ref, first_ref, second_ref, held, sems):
     depth = wa_ref.shape[0]
     copies = []
     for c in range(wa_ref.shape[1] // WIDE):
@@ -181,10 +214,7 @@
         copies[2 * c].wait()
         copies[2 * c + 1].wait()
         total = matmul(both, held[:, columns])
-        first = total[:BLOCK]
-        if len(refs) > 4:
-            first = first + refs[0][:, columns].astype(jnp.float32)
-        first_ref[:, columns] = first.astype(jnp.bfloat16)
+        first_ref[:, columns] = total[:BLOCK].astype(jnp.bfloat16)
         second_ref[:, columns] = total[BLOCK:].astype(jnp.bfloat16)
 
 
@@ -214,7 +244,6 @@
 def per_device(
     layer_input, norm_gain, projection_weight, output_weight, prompt_cache, subtree_cache, parents, leaf_scores
 ):
-    position = lax.axis_index("branch")
     nodes = lax.axis_size("branch")
     features = layer_input.shape[1]
 
@@ -254,25 +283,16 @@
     early_state = kernel(near_early, STATE, 16, 4 * QUERIES * PROMPT_TOKENS * HEAD_SIZE)(*early, prompt_cache)
 
     spread, early_state = lax.optimization_barrier((spread, early_state))
-    picked = kernel(pick, [(spread.shape, BF16)], 16, 1 << 22, (), [SMEM, VMEM])(parents, spread)[0]
+    shape = (nodes, 2 * spread.shape[1] + SPARE, HEAD_SIZE)
+    picked = kernel(pick, [(shape, BF16)], 16, 1 << 22, (), [SMEM, SMEM, VMEM])(parents, leaf_scores, spread)[0]
     context = lax.all_to_all(picked, "branch", 0, 0, tiled=True)
-    context = context.reshape(2 * SEGMENT_TOKENS, -1)
-    other_weight = tensor(lax.optimization_barrier((output_weight, early_state))[0], SWAP)
+    other_weight = tensor(output_weight, SWAP)
 
     late = run_project(1, x4, x3, x7, x6)
     depth = output_weight.shape[0]
     state = kernel(near_late, STATE + STATE, 20, 4 * QUERIES * (PROMPT_TOKENS + 2 * SEGMENT_TOKENS) * HEAD_SIZE)(
         prompt_cache, *early, *early_state, *late
     )
-
-    scores = jnp.broadcast_to(leaf_scores[:, None], (1, HEAD_SIZE))
-    for bit in range(5):
-        if bit == 1:
-            scores, state = lax.optimization_barrier((scores, state))
-        came = lax.ppermute(scores, "branch", [(b, b ^ (1 << bit)) for b in range(32)])
-        upper = (position >> bit) & 1 == 1
-        scores = jnp.where(upper, jnp.concatenate([came, scores]), jnp.concatenate([scores, came]))
-    scores = scores[:, 0]
 
     halves = [((ROWS // 2, 3 * HEAD_SIZE), BF16)] * 2
     run_far = kernel(far, halves, 16, 4 * QUERIES * 2 * SEGMENT_TOKENS * HEAD_SIZE)
@@ -283,7 +303,7 @@
         OUTPUT_MIB,
         8 * BLOCK * depth * features,
         [pltpu.VMEM((2 * depth, features), BF16), pltpu.SemaphoreType.DMA((2 * features // WIDE,))],
-        [VMEM, VMEM, ANY, ANY, VMEM][: len(args)],
+        [VMEM, VMEM, ANY, ANY],
     )(*args)
     late_mine, late_other = run_far(late[0], context, *state[3:])
     late_came = tensor(late_other, SWAP)
@@ -292,17 +312,13 @@
     y4, y3 = run_output(late_mine, late_came, output_weight, other_weight)
     z2 = tensor(y4, BACK)
     z1 = tensor(y3, BACK)
-    y2, y0 = run_output(early_mine, early_came, output_weight, other_weight, z2)
+    y2, y0 = run_output(early_mine, early_came, output_weight, other_weight)
+    run_join = lambda *terms: kernel(join, rows[:1], 8, 1 << 20)(*terms)[0]
+    y2 = run_join(y2, z2)
     z0 = tensor(y2, BACK)
+    least, product = kernel(tree, [((2, 1), F32)] * 2, 8, 1 << 20, (), [SMEM, VMEM])(parents, context)
     z1 = tensor(z1, SWAP)
-    attn_output = add(y0, z0, z1)
-
-    second = parents[1]
-    owners = jnp.stack([parents[0][second], second])
-    filled = jnp.where(owners == position, scores[None, :], 1.0)
-    subtree_min = jnp.min(filled, axis=1, keepdims=True)
-    subtree_product = jnp.prod(filled, axis=1, keepdims=True)
-    return attn_output, subtree_min, subtree_product
+    return add(y0, z0, z1), least, product
 
 
 def solution(mesh):

time: 107 us -> 94.1 us (0.88)
  the two profiles are of different devices: /device:TPU:8 before, /device:TPU:1 now
where the time goes in v2:
time: 94.1 us; the launch traced here: 93.8 us
  starting transfers between devices  35.2 us (37%)
  Pallas kernels  32.5 us (35%)
  waiting for transfers between devices  19.1 us (20%)
  other arithmetic  3.44 us (4%)
  local copies, waits for them, and re-layouts  1.98 us (2%)
  between operations  1.52 us (2%)
    pallas_call x11, Pallas kernels, kernel(): pl.pallas_call(body, in_specs=specs or [VMEM] * len(args), out_specs=[VME...  32.5 us
    ppermute x14, waiting for transfers between devices, tensor(): return lax.ppermute(x, 'tensor', pairs)  16.5 us
    ppermute x14, starting transfers between devices, tensor(): return lax.ppermute(x, 'tensor', pairs)  16.4 us
    all_to_all x1, starting transfers between devices, per_device(): spread = lax.all_to_all(pieces, 'branch', 0, 0, tiled=True)  11.2 us
    all_to_all x1, starting transfers between devices, per_device(): context = lax.all_to_all(picked, 'branch', 0, 0, tiled=True)  7.61 us
    convert_element_type x1, other arithmetic, add(): sum((term.astype(jnp.float32) for term in terms)).astype(jnp.bfloat16)  2.23 us
    all_to_all x1, waiting for transfers between devices, per_device(): spread = lax.all_to_all(pieces, 'branch', 0, 0, tiled=True)  2.07 us
    unnamed x18, local copies, waits for them, and re-layouts  1.98 us
  transfers between devices with their start and end apart: 16, of which 9 were waited for; matrix products, arithmetic and copies ran while one was open for 3% of the time, Pallas kernels for 29%

profile of v2, /device:TPU:1, one launch (start us, length us, event | category | flops | bytes accessed | tf_op | source)
XLA Modules:
  0.0 93.8 jit_solution(8842176438296510700)
XLA Ops:
  0.6 3.3 %collective-permute-start.8 = (bf16[384,5120]{1,0:T(8,128)(2,1)}, bf16[384,5120]{1,0:T(8,128)(2,1)}, u32[]{:S(2)}, u32[]{:S(2)}) collective-permute-start(bf16[384,5120]{1,0:T(8,128)(2,1)} %wa_ref.3), channel_id=1, source_target_pairs={{0,1},{1,0},{2,3},{3,2},{4,5},{5,4},{6,7},{7,6},{8,9},{9,8},{10,11... | collective-permute-start | bytes 11796488 | tf_op jit(solution)/shard_map/ppermute | solution.py:251
  3.9 0.8 collective-permute-start
  4.7 11.2 %all-to-all-start = ((bf16[32,32,256]{2,1,0:T(8,128)(2,1)}), bf16[32,32,256]{2,1,0:T(8,128)(2,1)S(1)}, u32[]{:S(2)}, u32[]{:S(2)}) async-start(bf16[32,32,256]{2,1,0:T(8,128)(2,1)} %bitcast.4), calls=%async_computation | async-start | bytes 1048576 | tf_op jit(solution)/shard_map/all_to_all | solution.py:263
  15.9 0.9 collective-permute-start.1
  16.8 0.6 collective-permute-start.3
  17.5 0.8 collective-permute-start.4
  18.2 1.0 %fusion = (f32[8,64,64]{2,1,0:T(8,128)S(1)}, f32[8,64,64]{2,1,0:T(8,128)S(1)}, f32[8,64,64]{2,1,0:T(8,128)S(1)}) fusion(f32[64]{0:T(128)S(1)} %multiply_power_fusion, f32[8,64]{1,0:T(8,128)S(1)} %add_convert_fusion.1), kind=kLoop, calls=%fused_computation.5 | loop fusion | flops 65536 | bytes 395520 | tf_op jit(solution)/shard_map/neg | solution.py:240
  20.1 4.4 %shard_map.103.qkv_ref.early_ref = bf16[5,256,128]{2,1,0:T(8,128)(2,1)S(1)} custom-call(bf16[64,5120]{1,0:T(8,128)(2,1)S(1)} %collective-permute-done.x0, bf16[64,5120]{1,0:T(8,128)(2,1)S(1)} %copy-done, bf16[64,5120]{1,0:T(8,128)(2,1)S(1)} %collective-permute-done.1.x2, bf16[64,5120]{1,0:T(8,128)(2,1)S(1)} %collective-permute-done.2.x3, ...), custom_call_target="tpu_custom_call" | custom-call | flops 1677721600 | bytes 1048576 | tf_op jit(solution)/shard_map/pallas_call | solution.py:43
  24.6 2.6 %shard_map.104 = (f32[1,768]{1,0:T(1,128)S(1)}, f32[1,768]{1,0:T(1,128)S(1)}, f32[128,768]{1,0:T(8,128)S(1)}) custom-call(bf16[5,256,128]{2,1,0:T(8,128)(2,1)S(1)} %shard_map.103.qkv_ref.early_ref, bf16[2048,256]{1,0:T(8,128)(2,1)S(1)} %copy-done.3), custom_call_target="tpu_custom_call" | custom-call | flops 805306368 | bytes 1048576 | tf_op jit(solution)/shard_map/pallas_call | solution.py:43
  27.2 0.7 copy-done.5
  28.0 2.1 %all-to-all-done.spread_ref = bf16[32,32,256]{2,1,0:T(8,128)(2,1)S(1)} async-done(((bf16[32,32,256]{2,1,0:T(8,128)(2,1)}), bf16[32,32,256]{2,1,0:T(8,128)(2,1)S(1)}, u32[]{:S(2)}, u32[]{:S(2)}) %all-to-all-start) | async-done | bytes 524320 | tf_op jit(solution)/shard_map/all_to_all | solution.py:263
  30.1 1.5 %shard_map.105 = bf16[32,72,128]{2,1,0:T(8,128)(2,1)} custom-call(s32[2,32]{1,0:T(2,128)S(1)} %copy-done.2, f32[1]{0:T(128)S(6)} %copy.13.score_ref, bf16[32,32,256]{2,1,0:T(8,128)(2,1)S(1)} %all-to-all-done.spread_ref), custom_call_target="tpu_custom_call" | custom-call | flops 4194304 | bytes 1048576 | tf_op jit(solution)/shard_map/pallas_call | solution.py:43
  31.6 7.6 %all-to-all-start.1 = ((bf16[32,72,128]{2,1,0:T(8,128)(2,1)}), bf16[32,72,128]{2,1,0:T(8,128)(2,1)S(1)}, u32[]{:S(2)}, u32[]{:S(2)}) async-start(bf16[32,72,128]{2,1,0:T(8,128)(2,1)} %shard_map.105), calls=%async_computation.1 | async-start | bytes 1179648 | tf_op jit(solution)/shard_map/all_to_all | solution.py:288
  39.2 1.9 %collective-permute-start.5 = (bf16[64,5120]{1,0:T(8,128)(2,1)S(1)}, bf16[64,5120]{1,0:T(8,128)(2,1)S(1)}, u32[]{:S(2)}, u32[]{:S(2)}) collective-permute-start(bf16[64,5120]{1,0:T(8,128)(2,1)S(1)} %collective-permute-done.3.x0), channel_id=1, source_target_pairs={{0,1},{1,0},{2,3},{3,2},{4,5},{5,4},{6,7},{7,6},{8,9},{9,8},{10,11... | collective-permute-start | bytes 1966088 | tf_op jit(solution)/shard_map/ppermute | solution.py:251
  41.3 1.6 %collective-permute-done.5.x2 = bf16[64,5120]{1,0:T(8,128)(2,1)S(1)} collective-permute-done((bf16[64,5120]{1,0:T(8,128)(2,1)S(1)}, bf16[64,5120]{1,0:T(8,128)(2,1)S(1)}, u32[]{:S(2)}, u32[]{:S(2)}) %collective-permute-start.5) | collective-permute-done | bytes 655392 | tf_op jit(solution)/shard_map/ppermute | solution.py:251
  42.9 0.9 collective-permute-done.6.x3
  43.8 5.4 %shard_map.106.late_ref.qkv_ref = bf16[5,256,128]{2,1,0:T(8,128)(2,1)S(1)} custom-call(bf16[64,5120]{1,0:T(8,128)(2,1)S(1)} %collective-permute-done.3.x0, bf16[64,5120]{1,0:T(8,128)(2,1)} %collective-permute-done.4.x1, bf16[64,5120]{1,0:T(8,128)(2,1)S(1)} %collective-permute-done.5.x2, bf16[64,5120]{1,0:T(8,128)(2,1)S(1)} %collective-permute-done.6.x3, ...), custom_call_target="tpu_custom_call" | custom-call | flops 1677721600 | bytes 1048576 | tf_op jit(solution)/shard_map/pallas_call | solution.py:43
  49.3 4.4 %shard_map.107 = (f32[1,768]{1,0:T(1,128)S(1)}, f32[1,768]{1,0:T(1,128)S(1)}, f32[128,768]{1,0:T(8,128)S(1)}, f32[1,768]{1,0:T(1,128)S(1)}, f32[1,768]{1,0:T(1,128)S(1)}, /*index=5*/f32[128,768]{1,0:T(8,128)S(1)}) custom-call(bf16[2048,256]{1,0:T(8,128)(2,1)S(1)} %copy-done.4, bf16[5,256,128]{2,1,0:T(8,128)(2,1)S(1)} %shard_map.103.qkv_ref.early_ref, ...), custom_call_target="tpu_custom_call" | custom-call | flops 1207959552 | bytes 1048576 | tf_op jit(solution)/shard_map/pallas_call | solution.py:43
  54.2 1.8 %shard_map.110 = (bf16[128,384]{1,0:T(8,128)(2,1)S(1)}, bf16[128,384]{1,0:T(8,128)(2,1)S(1)}) custom-call(bf16[5,256,128]{2,1,0:T(8,128)(2,1)S(1)} %shard_map.106.late_ref.qkv_ref, bf16[32,72,128]{2,1,0:T(8,128)(2,1)S(1)} %all-to-all-done.1.context_ref, f32[1,768]{1,0:T(1,128)S(1)} %get-tuple-element.40.top_ref, f32[1,768]{1,0:T(1,128)S(1)} %get-tuple-element.41.sum_ref, ...), custom_call_target="tpu_custom_call" | custom-call | flops 402653184 | bytes 1048576 | tf_op jit(solution)/shard_map/pallas_call | solution.py:43
  56.0 4.9 %collective-permute-start.9 = (bf16[128,384]{1,0:T(8,128)(2,1)S(1)}, bf16[128,384]{1,0:T(8,128)(2,1)S(1)}, u32[]{:S(2)}, u32[]{:S(2)}) collective-permute-start(bf16[128,384]{1,0:T(8,128)(2,1)S(1)} %get-tuple-element.44), channel_id=1, source_target_pairs={{0,1},{1,0},{2,3},{3,2},{4,5},{5,4},{6,7},{7,6},{8,9},{9,8},{10,11... | collective-permute-start | bytes 294920 | tf_op jit(solution)/shard_map/ppermute | solution.py:251
  60.9 0.9 %collective-permute-done.9.b_ref = bf16[128,384]{1,0:T(8,128)(2,1)S(1)} collective-permute-done((bf16[128,384]{1,0:T(8,128)(2,1)S(1)}, bf16[128,384]{1,0:T(8,128)(2,1)S(1)}, u32[]{:S(2)}, u32[]{:S(2)}) %collective-permute-start.9) | collective-permute-done | bytes 98336 | tf_op jit(solution)/shard_map/ppermute | solution.py:251
  61.9 4.9 %shard_map.111 = (bf16[64,5120]{1,0:T(8,128)(2,1)S(1)}, bf16[64,5120]{1,0:T(8,128)(2,1)}) custom-call(bf16[128,384]{1,0:T(8,128)(2,1)S(1)} %get-tuple-element.43.a_ref, bf16[128,384]{1,0:T(8,128)(2,1)S(1)} %collective-permute-done.9.b_ref, bf16[384,5120]{1,0:T(8,128)(2,1)} %wa_ref.3, bf16[384,5120]{1,0:T(8,128)(2,1)} %collective-permute-done.8.wb_ref), custom_call_target="tpu_custom_call" | custom-call | flops 1006632960 | bytes 1048576 | tf_op jit(solution)/shard_map/pallas_call | solution.py:43
  66.9 0.9 %collective-permute-start.12 = (bf16[64,5120]{1,0:T(8,128)(2,1)}, bf16[64,5120]{1,0:T(8,128)(2,1)S(1)}, u32[]{:S(2)}, u32[]{:S(2)}) collective-permute-start(bf16[64,5120]{1,0:T(8,128)(2,1)} %get-tuple-element.46), channel_id=1, source_target_pairs={{2,0},{7,1},{4,2},{1,3},{6,4},{3,5},{0,6},{5,7},{10,8},{15,9},{12,... | collective-permute-start | bytes 1966088 | tf_op jit(solution)/shard_map/ppermute | solution.py:251
  67.9 1.8 %shard_map.108 = (bf16[128,384]{1,0:T(8,128)(2,1)S(1)}, bf16[128,384]{1,0:T(8,128)(2,1)S(1)}) custom-call(bf16[5,256,128]{2,1,0:T(8,128)(2,1)S(1)} %shard_map.103.qkv_ref.early_ref, bf16[32,72,128]{2,1,0:T(8,128)(2,1)S(1)} %all-to-all-done.1.context_ref, f32[1,768]{1,0:T(1,128)S(1)} %get-tuple-element.33.top_ref, f32[1,768]{1,0:T(1,128)S(1)} %get-tuple-element.34.sum_ref, ...), custom_call_target="tpu_custom_call" | custom-call | flops 402653184 | bytes 1048576 | tf_op jit(solution)/shard_map/pallas_call | solution.py:43
  69.7 1.6 %collective-permute-start.7 = (bf16[128,384]{1,0:T(8,128)(2,1)S(1)}, bf16[128,384]{1,0:T(8,128)(2,1)S(1)}, u32[]{:S(2)}, u32[]{:S(2)}) collective-permute-start(bf16[128,384]{1,0:T(8,128)(2,1)S(1)} %get-tuple-element.37), channel_id=1, source_target_pairs={{0,1},{1,0},{2,3},{3,2},{4,5},{5,4},{6,7},{7,6},{8,9},{9,8},{10,11... | collective-permute-start | bytes 294920 | tf_op jit(solution)/shard_map/ppermute | solution.py:251
  71.3 0.9 %collective-permute-done.7.b_ref = bf16[128,384]{1,0:T(8,128)(2,1)S(1)} collective-permute-done((bf16[128,384]{1,0:T(8,128)(2,1)S(1)}, bf16[128,384]{1,0:T(8,128)(2,1)S(1)}, u32[]{:S(2)}, u32[]{:S(2)}) %collective-permute-start.7) | collective-permute-done | bytes 98336 | tf_op jit(solution)/shard_map/ppermute | solution.py:251
  72.2 4.9 %shard_map.109 = (bf16[64,5120]{1,0:T(8,128)(2,1)S(1)}, bf16[64,5120]{1,0:T(8,128)(2,1)}) custom-call(bf16[128,384]{1,0:T(8,128)(2,1)S(1)} %get-tuple-element.36.a_ref, bf16[128,384]{1,0:T(8,128)(2,1)S(1)} %collective-permute-done.7.b_ref, bf16[384,5120]{1,0:T(8,128)(2,1)} %wa_ref.3, bf16[384,5120]{1,0:T(8,128)(2,1)} %collective-permute-done.8.wb_ref), custom_call_target="tpu_custom_call" | custom-call | flops 1006632960 | bytes 1048576 | tf_op jit(solution)/shard_map/pallas_call | solution.py:43
  77.7 6.8 %collective-permute-done.12 = bf16[64,5120]{1,0:T(8,128)(2,1)S(1)} collective-permute-done((bf16[64,5120]{1,0:T(8,128)(2,1)}, bf16[64,5120]{1,0:T(8,128)(2,1)S(1)}, u32[]{:S(2)}, u32[]{:S(2)}) %collective-permute-start.12) | collective-permute-done | bytes 655392 | tf_op jit(solution)/shard_map/ppermute | solution.py:251
  84.8 0.6 shard_map.113
  85.4 0.6 copy.11
  86.6 4.9 %collective-permute-done.11 = bf16[64,5120]{1,0:T(8,128)(2,1)S(1)} collective-permute-done((bf16[64,5120]{1,0:T(8,128)(2,1)S(1)}, bf16[64,5120]{1,0:T(8,128)(2,1)S(1)}, u32[]{:S(2)}, u32[]{:S(2)}) %collective-permute-start.11) | collective-permute-done | bytes 655392 | tf_op jit(solution)/shard_map/ppermute | solution.py:251
  91.5 2.2 %add_convert_fusion = bf16[64,5120]{1,0:T(8,128)(2,1)} fusion(bf16[64,5120]{1,0:T(8,128)(2,1)} %collective-permute-done.13, bf16[64,5120]{1,0:T(8,128)(2,1)S(1)} %collective-permute-done.11, bf16[64,5120]{1,0:T(8,128)(2,1)S(1)} %copy-done.7), kind=kLoop, calls=%fused_computation | loop fusion | flops 1966080 | bytes 2621440 | tf_op jit(solution)/shard_map/convert_element_type | solution.py:228
  (34 shorter events, 2.6 us)
Async XLA Ops:
  0.6 61.2 %collective-permute-start.8 = (bf16[384,5120]{1,0:T(8,128)(2,1)}, bf16[384,5120]{1,0:T(8,128)(2,1)}, u32[]{:S(2)}, u32[]{:S(2)}) collective-permute-start(bf16[384,5120]{1,0:T(8,128)(2,1)} %wa_ref.3), channel_id=1, source_target_pairs={{0,1},{1,0},{2,3},{3,2},{4,5},{5,4},{6,7},{7,6},{8,9},{9,8},{10,11... | collective-permute-start | bytes 11796488 | tf_op jit(solution)/shard_map/ppermute | solution.py:251
  3.9 12.0 %collective-permute-start = (bf16[64,5120]{1,0:T(8,128)(2,1)}, bf16[64,5120]{1,0:T(8,128)(2,1)S(1)}, u32[]{:S(2)}, u32[]{:S(2)}) collective-permute-start(bf16[64,5120]{1,0:T(8,128)(2,1)} %x1.1), channel_id=1, source_target_pairs={{0,2},{1,7},{2,4},{3,1},{4,6},{5,3},{6,0},{7,5},{8,10},{9,15},{10,... | collective-permute-start | bytes 1966088 | tf_op jit(solution)/shard_map/ppermute | solution.py:251
  4.7 12.8 %collective-permute-start.2 = (bf16[64,5120]{1,0:T(8,128)(2,1)}, bf16[64,5120]{1,0:T(8,128)(2,1)S(1)}, u32[]{:S(2)}, u32[]{:S(2)}) collective-permute-start(bf16[64,5120]{1,0:T(8,128)(2,1)} %x1.1), channel_id=1, source_target_pairs={{0,1},{1,0},{2,3},{3,2},{4,5},{5,4},{6,7},{7,6},{8,9},{9,8},{10,11... | collective-permute-start | bytes 1966088 | tf_op jit(solution)/shard_map/ppermute | solution.py:251
  4.7 25.4 %all-to-all-start = ((bf16[32,32,256]{2,1,0:T(8,128)(2,1)}), bf16[32,32,256]{2,1,0:T(8,128)(2,1)S(1)}, u32[]{:S(2)}, u32[]{:S(2)}) async-start(bf16[32,32,256]{2,1,0:T(8,128)(2,1)} %bitcast.4), calls=%async_computation | async-start | bytes 1048576 | tf_op jit(solution)/shard_map/all_to_all | solution.py:263
  15.9 4.2 %copy-start = (bf16[64,5120]{1,0:T(8,128)(2,1)S(1)}, bf16[64,5120]{1,0:T(8,128)(2,1)}, u32[]{:S(2)}) copy-start(bf16[64,5120]{1,0:T(8,128)(2,1)} %x1.1) | copy-start | bytes 1966084
  15.9 4.2 %copy-start.1 = (f32[5120]{0:T(1024)S(1)}, f32[5120]{0:T(1024)}, u32[]{:S(2)}) copy-start(f32[5120]{0:T(1024)} %param.9) | copy-start | bytes 61444
  15.9 4.2 %collective-permute-start.1 = (bf16[64,5120]{1,0:T(8,128)(2,1)S(1)}, bf16[64,5120]{1,0:T(8,128)(2,1)S(1)}, u32[]{:S(2)}, u32[]{:S(2)}) collective-permute-start(bf16[64,5120]{1,0:T(8,128)(2,1)S(1)} %collective-permute-done.x0), channel_id=1, source_target_pairs={{0,1},{1,0},{2,3},{3,2},{4,5},{5,4},{6,7},{7,6},{8,9},{9,8},{10,11... | collective-permute-start | bytes 1966088 | tf_op jit(solution)/shard_map/ppermute | solution.py:251
  16.8 22.4 %collective-permute-start.3 = (bf16[64,5120]{1,0:T(8,128)(2,1)S(1)}, bf16[64,5120]{1,0:T(8,128)(2,1)S(1)}, u32[]{:S(2)}, u32[]{:S(2)}) collective-permute-start(bf16[64,5120]{1,0:T(8,128)(2,1)S(1)} %collective-permute-done.x0), channel_id=1, source_target_pairs={{0,2},{1,7},{2,4},{3,1},{4,6},{5,3},{6,0},{7,5},{8,10},{9,15},{10,... | collective-permute-start | bytes 1966088 | tf_op jit(solution)/shard_map/ppermute | solution.py:251
  17.5 23.7 %collective-permute-start.4 = (bf16[64,5120]{1,0:T(8,128)(2,1)S(1)}, bf16[64,5120]{1,0:T(8,128)(2,1)}, u32[]{:S(2)}, u32[]{:S(2)}) collective-permute-start(bf16[64,5120]{1,0:T(8,128)(2,1)S(1)} %collective-permute-done.2.x3), channel_id=1, source_target_pairs={{0,2},{1,7},{2,4},{3,1},{4,6},{5,3},{6,0},{7,5},{8,10},{9,15},{10,... | collective-permute-start | bytes 1966088 | tf_op jit(solution)/shard_map/ppermute | solution.py:251
  20.1 4.5 %copy-start.3 = (bf16[2048,256]{1,0:T(8,128)(2,1)S(1)}, bf16[2048,256]{1,0:T(8,128)(2,1)}, u32[]{:S(2)}) copy-start(bf16[2048,256]{1,0:T(8,128)(2,1)} %prompt_ref.3) | copy-start | bytes 3145732
  24.6 5.5 %copy-start.2 = (s32[2,32]{1,0:T(2,128)S(1)}, s32[2,32]{1,0:T(2,128)}, u32[]{:S(2)}) copy-start(s32[2,32]{1,0:T(2,128)} %parents_ref.3) | copy-start | bytes 772
  27.2 0.8 copy-start.5
  31.6 22.7 %all-to-all-start.1 = ((bf16[32,72,128]{2,1,0:T(8,128)(2,1)}), bf16[32,72,128]{2,1,0:T(8,128)(2,1)S(1)}, u32[]{:S(2)}, u32[]{:S(2)}) async-start(bf16[32,72,128]{2,1,0:T(8,128)(2,1)} %shard_map.105), calls=%async_computation.1 | async-start | bytes 1179648 | tf_op jit(solution)/shard_map/all_to_all | solution.py:288
  39.2 10.1 %copy-start.4 = (bf16[2048,256]{1,0:T(8,128)(2,1)S(1)}, bf16[2048,256]{1,0:T(8,128)(2,1)}, u32[]{:S(2)}) copy-start(bf16[2048,256]{1,0:T(8,128)(2,1)} %prompt_ref.3) | copy-start | bytes 3145732
  39.2 10.1 %copy-start.6 = (f32[128,768]{1,0:T(8,128)S(1)}, f32[128,768]{1,0:T(8,128)}, u32[]{:S(2)}) copy-start(f32[128,768]{1,0:T(8,128)} %copy-done.5) | copy-start | bytes 1179652
  39.2 3.7 %collective-permute-start.5 = (bf16[64,5120]{1,0:T(8,128)(2,1)S(1)}, bf16[64,5120]{1,0:T(8,128)(2,1)S(1)}, u32[]{:S(2)}, u32[]{:S(2)}) collective-permute-start(bf16[64,5120]{1,0:T(8,128)(2,1)S(1)} %collective-permute-done.3.x0), channel_id=1, source_target_pairs={{0,1},{1,0},{2,3},{3,2},{4,5},{5,4},{6,7},{7,6},{8,9},{9,8},{10,11... | collective-permute-start | bytes 1966088 | tf_op jit(solution)/shard_map/ppermute | solution.py:251
  41.1 2.7 %collective-permute-start.6 = (bf16[64,5120]{1,0:T(8,128)(2,1)}, bf16[64,5120]{1,0:T(8,128)(2,1)S(1)}, u32[]{:S(2)}, u32[]{:S(2)}) collective-permute-start(bf16[64,5120]{1,0:T(8,128)(2,1)} %collective-permute-done.4.x1), channel_id=1, source_target_pairs={{0,1},{1,0},{2,3},{3,2},{4,5},{5,4},{6,7},{7,6},{8,9},{9,8},{10,11... | collective-permute-start | bytes 1966088 | tf_op jit(solution)/shard_map/ppermute | solution.py:251
  56.0 5.8 %collective-permute-start.9 = (bf16[128,384]{1,0:T(8,128)(2,1)S(1)}, bf16[128,384]{1,0:T(8,128)(2,1)S(1)}, u32[]{:S(2)}, u32[]{:S(2)}) collective-permute-start(bf16[128,384]{1,0:T(8,128)(2,1)S(1)} %get-tuple-element.44), channel_id=1, source_target_pairs={{0,1},{1,0},{2,3},{3,2},{4,5},{5,4},{6,7},{7,6},{8,9},{9,8},{10,11... | collective-permute-start | bytes 294920 | tf_op jit(solution)/shard_map/ppermute | solution.py:251
  66.8 10.7 %collective-permute-start.10 = (bf16[64,5120]{1,0:T(8,128)(2,1)S(1)}, bf16[64,5120]{1,0:T(8,128)(2,1)S(1)}, u32[]{:S(2)}, u32[]{:S(2)}) collective-permute-start(bf16[64,5120]{1,0:T(8,128)(2,1)S(1)} %get-tuple-element.45), channel_id=1, source_target_pairs={{2,0},{7,1},{4,2},{1,3},{6,4},{3,5},{0,6},{5,7},{10,8},{15,9},{12,... | collective-permute-start | bytes 1966088 | tf_op jit(solution)/shard_map/ppermute | solution.py:251
  66.9 17.5 %collective-permute-start.12 = (bf16[64,5120]{1,0:T(8,128)(2,1)}, bf16[64,5120]{1,0:T(8,128)(2,1)S(1)}, u32[]{:S(2)}, u32[]{:S(2)}) collective-permute-start(bf16[64,5120]{1,0:T(8,128)(2,1)} %get-tuple-element.46), channel_id=1, source_target_pairs={{2,0},{7,1},{4,2},{1,3},{6,4},{3,5},{0,6},{5,7},{10,8},{15,9},{12,... | collective-permute-start | bytes 1966088 | tf_op jit(solution)/shard_map/ppermute | solution.py:251
  69.7 2.6 %collective-permute-start.7 = (bf16[128,384]{1,0:T(8,128)(2,1)S(1)}, bf16[128,384]{1,0:T(8,128)(2,1)S(1)}, u32[]{:S(2)}, u32[]{:S(2)}) collective-permute-start(bf16[128,384]{1,0:T(8,128)(2,1)S(1)} %get-tuple-element.37), channel_id=1, source_target_pairs={{0,1},{1,0},{2,3},{3,2},{4,5},{5,4},{6,7},{7,6},{8,9},{9,8},{10,11... | collective-permute-start | bytes 294920 | tf_op jit(solution)/shard_map/ppermute | solution.py:251
  77.1 14.4 %copy-start.7 = (bf16[64,5120]{1,0:T(8,128)(2,1)S(1)}, bf16[64,5120]{1,0:T(8,128)(2,1)}, u32[]{:S(2)}) copy-start(bf16[64,5120]{1,0:T(8,128)(2,1)} %get-tuple-element.38) | copy-start | bytes 1966084
  77.6 13.9 %collective-permute-start.11 = (bf16[64,5120]{1,0:T(8,128)(2,1)S(1)}, bf16[64,5120]{1,0:T(8,128)(2,1)S(1)}, u32[]{:S(2)}, u32[]{:S(2)}) collective-permute-start(bf16[64,5120]{1,0:T(8,128)(2,1)S(1)} %shard_map.112), channel_id=1, source_target_pairs={{2,0},{7,1},{4,2},{1,3},{6,4},{3,5},{0,6},{5,7},{10,8},{15,9},{12,... | collective-permute-start | bytes 1966088 | tf_op jit(solution)/shard_map/ppermute | solution.py:251
  84.5 7.0 %collective-permute-start.13 = (bf16[64,5120]{1,0:T(8,128)(2,1)S(1)}, bf16[64,5120]{1,0:T(8,128)(2,1)}, u32[]{:S(2)}, u32[]{:S(2)}) collective-permute-start(bf16[64,5120]{1,0:T(8,128)(2,1)S(1)} %collective-permute-done.12), channel_id=1, source_target_pairs={{0,1},{1,0},{2,3},{3,2},{4,5},{5,4},{6,7},{7,6},{8,9},{9,8},{10,11... | collective-permute-start | bytes 1966088 | tf_op jit(solution)/shard_map/ppermute | solution.py:251

commit v3 on v2

--- a/solution.py
+++ b/solution.py
@@ -18,7 +18,6 @@
 BLOCK = 64
 ROWS = 256
 DEPTH = 1024
-WIDE = 2560
 SPARE = 8
 CHUNK = 512
 
@@ -148,9 +147,11 @@
         product_ref[level : level + 1, :] = product[:, :1]
 
 
-def join(*refs):
-    total = sum(ref[...].astype(jnp.float32) for ref in refs[:-1])
-    refs[-1][...] = total.astype(refs[-1].dtype)
+def join(block_ref, left_ref, right_ref, sum_ref):
+    half = left_ref.shape[1]
+    for columns, ref in ((slice(0, half), left_ref), (slice(half, 2 * half), right_ref)):
+        total = block_ref[:, columns].astype(jnp.float32) + ref[...].astype(jnp.float32)
+        sum_ref[:, columns] = total.astype(sum_ref.dtype)
 
 
 def prompt_part(state, q, prompt_ref):
@@ -199,33 +200,31 @@
         other_ref[:, columns] = mixed[head * ROWS + ROWS // 2 : (head + 1) * ROWS]
 
 
-def output(a_ref, b_ref, wa_ref, wb_ref, first_ref, second_ref, held, sems):
+def output(first, wide, a_ref, b_ref, wa_ref, wb_ref, first_ref, second_ref, held, sems):
     depth = wa_ref.shape[0]
+    steps = held.shape[1] // wide
     copies = []
-    for c in range(wa_ref.shape[1] // WIDE):
-        columns = slice(c * WIDE, (c + 1) * WIDE)
-        copies.append(pltpu.make_async_copy(wa_ref.at[:, columns], held.at[:depth, columns], sems.at[2 * c]))
-        copies.append(pltpu.make_async_copy(wb_ref.at[:, columns], held.at[depth:, columns], sems.at[2 * c + 1]))
+    for c in range(steps):
+        here = slice(c * wide, (c + 1) * wide)
+        there = slice(first + c * wide, first + (c + 1) * wide)
+        copies.append(pltpu.make_async_copy(wa_ref.at[:, there], held.at[:depth, here], sems.at[2 * c]))
+        copies.append(pltpu.make_async_copy(wb_ref.at[:, there], held.at[depth:, here], sems.at[2 * c + 1]))
     for copy in copies:
         copy.start()
     both = jnp.concatenate([a_ref[...], b_ref[...]], 1)
-    for c in range(wa_ref.shape[1] // WIDE):
-        columns = slice(c * WIDE, (c + 1) * WIDE)
+    for c in range(steps):
+        here = slice(c * wide, (c + 1) * wide)
         copies[2 * c].wait()
         copies[2 * c + 1].wait()
-        total = matmul(both, held[:, columns])
-        first_ref[:, columns] = total[:BLOCK].astype(jnp.bfloat16)
-        second_ref[:, columns] = total[BLOCK:].astype(jnp.bfloat16)
+        total = matmul(both, held[:, here])
+        first_ref[:, here] = total[:BLOCK].astype(jnp.bfloat16)
+        second_ref[:, here] = total[BLOCK:].astype(jnp.bfloat16)
 
 
 QUERIES = 3 * ROWS
 PROJECT_MIB, OUTPUT_MIB = 50, 53
 F32, BF16 = jnp.float32, jnp.bfloat16
 STATE = [((1, QUERIES), F32), ((1, QUERIES), F32), ((HEAD_SIZE, QUERIES), F32)]
-
-
-def add(*terms):
-    return sum(term.astype(jnp.float32) for term in terms).astype(jnp.bfloat16)
 
 
 def tables():
@@ -296,29 +295,36 @@
 
     halves = [((ROWS // 2, 3 * HEAD_SIZE), BF16)] * 2
     run_far = kernel(far, halves, 16, 4 * QUERIES * 2 * SEGMENT_TOKENS * HEAD_SIZE)
-    rows = [((BLOCK, features), BF16)] * 2
-    run_output = lambda *args: kernel(
-        output,
-        rows,
-        OUTPUT_MIB,
-        8 * BLOCK * depth * features,
-        [pltpu.VMEM((2 * depth, features), BF16), pltpu.SemaphoreType.DMA((2 * features // WIDE,))],
-        [VMEM, VMEM, ANY, ANY],
-    )(*args)
+    depth = output_weight.shape[0]
+
+    def run_output(first, count, a, b):
+        return kernel(
+            functools.partial(output, first, count // 2),
+            [((BLOCK, count), BF16)] * 2,
+            OUTPUT_MIB,
+            8 * BLOCK * depth * count,
+            [pltpu.VMEM((2 * depth, count), BF16), pltpu.SemaphoreType.DMA((4,))],
+            [VMEM, VMEM, ANY, ANY],
+        )(a, b, output_weight, other_weight)
+
+    half = features // 2
     late_mine, late_other = run_far(late[0], context, *state[3:])
     late_came = tensor(late_other, SWAP)
     early_mine, early_other = run_far(early[0], context, *state[:3])
     early_came = tensor(early_other, SWAP)
-    y4, y3 = run_output(late_mine, late_came, output_weight, other_weight)
-    z2 = tensor(y4, BACK)
-    z1 = tensor(y3, BACK)
-    y2, y0 = run_output(early_mine, early_came, output_weight, other_weight)
-    run_join = lambda *terms: kernel(join, rows[:1], 8, 1 << 20)(*terms)[0]
-    y2 = run_join(y2, z2)
+    z1, z2 = [], []
+    for i in range(2):
+        y4, y3 = run_output(i * half, half, late_mine, late_came)
+        z2.append(tensor(y4, BACK))
+        z1.append(tensor(y3, BACK))
+    y2, y0 = run_output(0, features, early_mine, early_came)
+    y2 = kernel(join, [((BLOCK, features), BF16)], 8, 1 << 20)(y2, *z2)[0]
     z0 = tensor(y2, BACK)
     least, product = kernel(tree, [((2, 1), F32)] * 2, 8, 1 << 20, (), [SMEM, VMEM])(parents, context)
-    z1 = tensor(z1, SWAP)
-    return add(y0, z0, z1), least, product
+    z1 = [tensor(part, SWAP) for part in z1]
+    own = kernel(join, [((BLOCK, features), F32)], 8, 1 << 20)(y0, *z1)[0]
+    attn_output = (own + z0.astype(F32)).astype(BF16)
+    return attn_output, least, product
 
 
 def solution(mesh):

time: 94.1 us -> 90.9 us (0.966)
  waiting for transfers between devices: 19.1 us -> 13.6 us
  starting transfers between devices: 35.2 us -> 38.2 us
  other arithmetic: 3.44 us -> 2.2 us
    ppermute x14 -> x17, waiting for transfers between devices: 16.5 us -> 11 us  [tensor(): return lax.ppermute(x, 'tensor', pairs)]
    ppermute x14 -> x17, starting transfers between devices: 16.4 us -> 19.4 us  [tensor(): return lax.ppermute(x, 'tensor', pairs)]
    convert_element_type x1, other arithmetic: 2.23 us -> 0.99 us  [per_device(): attn_output = (own + z0.astype(F32)).astype(BF16)]
    pallas_call x11 -> x13, Pallas kernels: 32.5 us -> 33 us  [kernel(): pl.pallas_call(body, in_specs=specs or [VMEM] * len(args), out_specs=[VME...]
  transfers between devices with their start and end apart: 16 -> 19, of which waited for: 9 -> 8; matrix products, arithmetic and copies ran while one was open for 3% -> 3% of each run, Pallas kernels for 29% -> 34%
where the time goes in v3:
time: 90.9 us; the launch traced here: 90.6 us
  starting transfers between devices  38.2 us (42%)
  Pallas kernels  33 us (36%)
  waiting for transfers between devices  13.6 us (15%)
  other arithmetic  2.2 us (2%)
  local copies, waits for them, and re-layouts  1.98 us (2%)
  between operations  1.56 us (2%)
    pallas_call x13, Pallas kernels, kernel(): pl.pallas_call(body, in_specs=specs or [VMEM] * len(args), out_specs=[VME...  33 us
    ppermute x17, starting transfers between devices, tensor(): return lax.ppermute(x, 'tensor', pairs)  19.4 us
    all_to_all x1, starting transfers between devices, per_device(): spread = lax.all_to_all(pieces, 'branch', 0, 0, tiled=True)  11.2 us
    ppermute x17, waiting for transfers between devices, tensor(): return lax.ppermute(x, 'tensor', pairs)  11 us
    all_to_all x1, starting transfers between devices, per_device(): context = lax.all_to_all(picked, 'branch', 0, 0, tiled=True)  7.61 us
    all_to_all x1, waiting for transfers between devices, per_device(): spread = lax.all_to_all(pieces, 'branch', 0, 0, tiled=True)  2.08 us
    unnamed x18, local copies, waits for them, and re-layouts  1.98 us
  transfers between devices with their start and end apart: 19, of which 8 were waited for; matrix products, arithmetic and copies ran while one was open for 3% of the time, Pallas kernels for 34%

profile of v3, /device:TPU:1, one launch (start us, length us, event | category | flops | bytes accessed | tf_op | source)
XLA Modules:
  0.0 90.6 jit_solution(6498813245529477193)
XLA Ops:
  0.6 3.3 %collective-permute-start.8 = (bf16[384,5120]{1,0:T(8,128)(2,1)}, bf16[384,5120]{1,0:T(8,128)(2,1)}, u32[]{:S(2)}, u32[]{:S(2)}) collective-permute-start(bf16[384,5120]{1,0:T(8,128)(2,1)} %wa_ref.5), channel_id=1, source_target_pairs={{0,1},{1,0},{2,3},{3,2},{4,5},{5,4},{6,7},{7,6},{8,9},{9,8},{10,11... | collective-permute-start | bytes 11796488 | tf_op jit(solution)/shard_map/ppermute | solution.py:250
  3.9 0.8 collective-permute-start
  4.7 11.2 %all-to-all-start = ((bf16[32,32,256]{2,1,0:T(8,128)(2,1)}), bf16[32,32,256]{2,1,0:T(8,128)(2,1)S(1)}, u32[]{:S(2)}, u32[]{:S(2)}) async-start(bf16[32,32,256]{2,1,0:T(8,128)(2,1)} %bitcast.4), calls=%async_computation | async-start | bytes 1048576 | tf_op jit(solution)/shard_map/all_to_all | solution.py:262
  15.9 0.9 collective-permute-start.1
  17.5 0.8 collective-permute-start.4
  18.2 1.0 %fusion = (f32[8,64,64]{2,1,0:T(8,128)S(1)}, f32[8,64,64]{2,1,0:T(8,128)S(1)}, f32[8,64,64]{2,1,0:T(8,128)S(1)}) fusion(f32[64]{0:T(128)S(1)} %multiply_power_fusion, f32[8,64]{1,0:T(8,128)S(1)} %add_convert_fusion.1), kind=kLoop, calls=%fused_computation.5 | loop fusion | flops 65536 | bytes 395520 | tf_op jit(solution)/shard_map/neg | solution.py:239
  20.1 4.4 %shard_map.103.qkv_ref.early_ref = bf16[5,256,128]{2,1,0:T(8,128)(2,1)S(1)} custom-call(bf16[64,5120]{1,0:T(8,128)(2,1)S(1)} %collective-permute-done.x0, bf16[64,5120]{1,0:T(8,128)(2,1)S(1)} %copy-done, bf16[64,5120]{1,0:T(8,128)(2,1)S(1)} %collective-permute-done.1.x2, bf16[64,5120]{1,0:T(8,128)(2,1)S(1)} %collective-permute-done.2.x3, ...), custom_call_target="tpu_custom_call" | custom-call | flops 1677721600 | bytes 1048576 | tf_op jit(solution)/shard_map/pallas_call | solution.py:42
  24.6 2.6 %shard_map.104 = (f32[1,768]{1,0:T(1,128)S(1)}, f32[1,768]{1,0:T(1,128)S(1)}, f32[128,768]{1,0:T(8,128)S(1)}) custom-call(bf16[5,256,128]{2,1,0:T(8,128)(2,1)S(1)} %shard_map.103.qkv_ref.early_ref, bf16[2048,256]{1,0:T(8,128)(2,1)S(1)} %copy-done.4), custom_call_target="tpu_custom_call" | custom-call | flops 805306368 | bytes 1048576 | tf_op jit(solution)/shard_map/pallas_call | solution.py:42
  27.2 0.7 copy-done.6
  28.0 2.1 %all-to-all-done.spread_ref = bf16[32,32,256]{2,1,0:T(8,128)(2,1)S(1)} async-done(((bf16[32,32,256]{2,1,0:T(8,128)(2,1)}), bf16[32,32,256]{2,1,0:T(8,128)(2,1)S(1)}, u32[]{:S(2)}, u32[]{:S(2)}) %all-to-all-start) | async-done | bytes 524320 | tf_op jit(solution)/shard_map/all_to_all | solution.py:262
  30.1 1.5 %shard_map.105 = bf16[32,72,128]{2,1,0:T(8,128)(2,1)} custom-call(s32[2,32]{1,0:T(2,128)S(1)} %copy-done.3, f32[1]{0:T(128)S(6)} %copy.13.score_ref, bf16[32,32,256]{2,1,0:T(8,128)(2,1)S(1)} %all-to-all-done.spread_ref), custom_call_target="tpu_custom_call" | custom-call | flops 4194304 | bytes 1048576 | tf_op jit(solution)/shard_map/pallas_call | solution.py:42
  31.6 7.6 %all-to-all-start.1 = ((bf16[32,72,128]{2,1,0:T(8,128)(2,1)}), bf16[32,72,128]{2,1,0:T(8,128)(2,1)S(1)}, u32[]{:S(2)}, u32[]{:S(2)}) async-start(bf16[32,72,128]{2,1,0:T(8,128)(2,1)} %shard_map.105), calls=%async_computation.1 | async-start | bytes 1179648 | tf_op jit(solution)/shard_map/all_to_all | solution.py:287
  39.2 1.9 %collective-permute-start.5 = (bf16[64,5120]{1,0:T(8,128)(2,1)S(1)}, bf16[64,5120]{1,0:T(8,128)(2,1)S(1)}, u32[]{:S(2)}, u32[]{:S(2)}) collective-permute-start(bf16[64,5120]{1,0:T(8,128)(2,1)S(1)} %collective-permute-done.3.x0), channel_id=1, source_target_pairs={{0,1},{1,0},{2,3},{3,2},{4,5},{5,4},{6,7},{7,6},{8,9},{9,8},{10,11... | collective-permute-start | bytes 1966088 | tf_op jit(solution)/shard_map/ppermute | solution.py:250
  41.3 1.6 %collective-permute-done.5.x2 = bf16[64,5120]{1,0:T(8,128)(2,1)S(1)} collective-permute-done((bf16[64,5120]{1,0:T(8,128)(2,1)S(1)}, bf16[64,5120]{1,0:T(8,128)(2,1)S(1)}, u32[]{:S(2)}, u32[]{:S(2)}) %collective-permute-start.5) | collective-permute-done | bytes 655392 | tf_op jit(solution)/shard_map/ppermute | solution.py:250
  42.9 0.9 %collective-permute-done.6.x3 = bf16[64,5120]{1,0:T(8,128)(2,1)S(1)} collective-permute-done((bf16[64,5120]{1,0:T(8,128)(2,1)}, bf16[64,5120]{1,0:T(8,128)(2,1)S(1)}, u32[]{:S(2)}, u32[]{:S(2)}) %collective-permute-start.6) | collective-permute-done | bytes 655392 | tf_op jit(solution)/shard_map/ppermute | solution.py:250
  43.8 5.4 %shard_map.106.late_ref.qkv_ref = bf16[5,256,128]{2,1,0:T(8,128)(2,1)S(1)} custom-call(bf16[64,5120]{1,0:T(8,128)(2,1)S(1)} %collective-permute-done.3.x0, bf16[64,5120]{1,0:T(8,128)(2,1)} %collective-permute-done.4.x1, bf16[64,5120]{1,0:T(8,128)(2,1)S(1)} %collective-permute-done.5.x2, bf16[64,5120]{1,0:T(8,128)(2,1)S(1)} %collective-permute-done.6.x3, ...), custom_call_target="tpu_custom_call" | custom-call | flops 1677721600 | bytes 1048576 | tf_op jit(solution)/shard_map/pallas_call | solution.py:42
  49.3 4.4 %shard_map.107 = (f32[1,768]{1,0:T(1,128)S(1)}, f32[1,768]{1,0:T(1,128)S(1)}, f32[128,768]{1,0:T(8,128)S(1)}, f32[1,768]{1,0:T(1,128)S(1)}, f32[1,768]{1,0:T(1,128)S(1)}, /*index=5*/f32[128,768]{1,0:T(8,128)S(1)}) custom-call(bf16[2048,256]{1,0:T(8,128)(2,1)S(1)} %copy-done.5, bf16[5,256,128]{2,1,0:T(8,128)(2,1)S(1)} %shard_map.103.qkv_ref.early_ref, ...), custom_call_target="tpu_custom_call" | custom-call | flops 1207959552 | bytes 1048576 | tf_op jit(solution)/shard_map/pallas_call | solution.py:42
  54.2 1.8 %shard_map.110 = (bf16[128,384]{1,0:T(8,128)(2,1)S(1)}, bf16[128,384]{1,0:T(8,128)(2,1)S(1)}) custom-call(bf16[5,256,128]{2,1,0:T(8,128)(2,1)S(1)} %shard_map.106.late_ref.qkv_ref, bf16[32,72,128]{2,1,0:T(8,128)(2,1)S(1)} %all-to-all-done.1.context_ref, f32[1,768]{1,0:T(1,128)S(1)} %get-tuple-element.41.top_ref, f32[1,768]{1,0:T(1,128)S(1)} %get-tuple-element.42.sum_ref, ...), custom_call_target="tpu_custom_call" | custom-call | flops 402653184 | bytes 1048576 | tf_op jit(solution)/shard_map/pallas_call | solution.py:42
  56.0 4.9 %collective-permute-start.9 = (bf16[128,384]{1,0:T(8,128)(2,1)S(1)}, bf16[128,384]{1,0:T(8,128)(2,1)S(1)}, u32[]{:S(2)}, u32[]{:S(2)}) collective-permute-start(bf16[128,384]{1,0:T(8,128)(2,1)S(1)} %get-tuple-element.45), channel_id=1, source_target_pairs={{0,1},{1,0},{2,3},{3,2},{4,5},{5,4},{6,7},{7,6},{8,9},{9,8},{10,11... | collective-permute-start | bytes 294920 | tf_op jit(solution)/shard_map/ppermute | solution.py:250
  60.9 0.9 %collective-permute-done.9.b_ref = bf16[128,384]{1,0:T(8,128)(2,1)S(1)} collective-permute-done((bf16[128,384]{1,0:T(8,128)(2,1)S(1)}, bf16[128,384]{1,0:T(8,128)(2,1)S(1)}, u32[]{:S(2)}, u32[]{:S(2)}) %collective-permute-start.9) | collective-permute-done | bytes 98336 | tf_op jit(solution)/shard_map/ppermute | solution.py:250
  61.9 2.6 %shard_map.112 = (bf16[64,2560]{1,0:T(8,128)(2,1)S(1)}, bf16[64,2560]{1,0:T(8,128)(2,1)S(1)}) custom-call(bf16[128,384]{1,0:T(8,128)(2,1)S(1)} %get-tuple-element.44.a_ref, bf16[128,384]{1,0:T(8,128)(2,1)S(1)} %collective-permute-done.9.b_ref, bf16[384,5120]{1,0:T(8,128)(2,1)} %wa_ref.5, bf16[384,5120]{1,0:T(8,128)(2,1)} %collective-permute-done.8.wb_ref), custom_call_target="tpu_custom_call" | custom-call | flops 503316480 | bytes 1048576 | tf_op jit(solution)/shard_map/pallas_call | solution.py:42
  64.7 2.6 %shard_map.111 = (bf16[64,2560]{1,0:T(8,128)(2,1)S(1)}, bf16[64,2560]{1,0:T(8,128)(2,1)S(1)}) custom-call(bf16[128,384]{1,0:T(8,128)(2,1)S(1)} %get-tuple-element.44.a_ref, bf16[128,384]{1,0:T(8,128)(2,1)S(1)} %collective-permute-done.9.b_ref, bf16[384,5120]{1,0:T(8,128)(2,1)} %wa_ref.5, bf16[384,5120]{1,0:T(8,128)(2,1)} %collective-permute-done.8.wb_ref), custom_call_target="tpu_custom_call" | custom-call | flops 503316480 | bytes 1048576 | tf_op jit(solution)/shard_map/pallas_call | solution.py:42
  67.3 1.2 %collective-permute-start.14 = (bf16[64,2560]{1,0:T(8,128)(2,1)S(1)}, bf16[64,2560]{1,0:T(8,128)(2,1)S(1)}, u32[]{:S(2)}, u32[]{:S(2)}) collective-permute-start(bf16[64,2560]{1,0:T(8,128)(2,1)S(1)} %get-tuple-element.49), channel_id=1, source_target_pairs={{2,0},{7,1},{4,2},{1,3},{6,4},{3,5},{0,6},{5,7},{10,8},{15,9},{12,... | collective-permute-start | bytes 983048 | tf_op jit(solution)/shard_map/ppermute | solution.py:250
  68.5 1.8 %shard_map.108 = (bf16[128,384]{1,0:T(8,128)(2,1)S(1)}, bf16[128,384]{1,0:T(8,128)(2,1)S(1)}) custom-call(bf16[5,256,128]{2,1,0:T(8,128)(2,1)S(1)} %shard_map.103.qkv_ref.early_ref, bf16[32,72,128]{2,1,0:T(8,128)(2,1)S(1)} %all-to-all-done.1.context_ref, f32[1,768]{1,0:T(1,128)S(1)} %get-tuple-element.35.top_ref, f32[1,768]{1,0:T(1,128)S(1)} %get-tuple-element.36.sum_ref, ...), custom_call_target="tpu_custom_call" | custom-call | flops 402653184 | bytes 1048576 | tf_op jit(solution)/shard_map/pallas_call | solution.py:42
  70.3 1.6 %collective-permute-start.7 = (bf16[128,384]{1,0:T(8,128)(2,1)S(1)}, bf16[128,384]{1,0:T(8,128)(2,1)S(1)}, u32[]{:S(2)}, u32[]{:S(2)}) collective-permute-start(bf16[128,384]{1,0:T(8,128)(2,1)S(1)} %get-tuple-element.39), channel_id=1, source_target_pairs={{0,1},{1,0},{2,3},{3,2},{4,5},{5,4},{6,7},{7,6},{8,9},{9,8},{10,11... | collective-permute-start | bytes 294920 | tf_op jit(solution)/shard_map/ppermute | solution.py:250
  72.3 0.9 collective-permute-start.10
  73.2 4.9 %shard_map.109 = (bf16[64,5120]{1,0:T(8,128)(2,1)S(1)}, bf16[64,5120]{1,0:T(8,128)(2,1)}) custom-call(bf16[128,384]{1,0:T(8,128)(2,1)S(1)} %get-tuple-element.38.a_ref, bf16[128,384]{1,0:T(8,128)(2,1)S(1)} %collective-permute-done.7.b_ref, bf16[384,5120]{1,0:T(8,128)(2,1)} %wa_ref.5, bf16[384,5120]{1,0:T(8,128)(2,1)} %collective-permute-done.8.wb_ref), custom_call_target="tpu_custom_call" | custom-call | flops 1006632960 | bytes 1048576 | tf_op jit(solution)/shard_map/pallas_call | solution.py:42
  79.1 1.4 %collective-permute-start.13 = (bf16[64,2560]{1,0:T(8,128)(2,1)S(1)}, bf16[64,2560]{1,0:T(8,128)(2,1)S(1)}, u32[]{:S(2)}, u32[]{:S(2)}) collective-permute-start(bf16[64,2560]{1,0:T(8,128)(2,1)S(1)} %collective-permute-done.12), channel_id=1, source_target_pairs={{0,1},{1,0},{2,3},{3,2},{4,5},{5,4},{6,7},{7,6},{8,9},{9,8},{10,11... | collective-permute-start | bytes 983048 | tf_op jit(solution)/shard_map/ppermute | solution.py:250
  80.5 2.2 %collective-permute-done.10 = bf16[64,2560]{1,0:T(8,128)(2,1)} collective-permute-done((bf16[64,2560]{1,0:T(8,128)(2,1)S(1)}, bf16[64,2560]{1,0:T(8,128)(2,1)}, u32[]{:S(2)}, u32[]{:S(2)}) %collective-permute-start.10) | collective-permute-done | bytes 327712 | tf_op jit(solution)/shard_map/ppermute | solution.py:250
  82.9 0.6 shard_map.115
  84.9 4.7 %collective-permute-done.16 = bf16[64,5120]{1,0:T(8,128)(2,1)S(1)} collective-permute-done((bf16[64,5120]{1,0:T(8,128)(2,1)S(1)}, bf16[64,5120]{1,0:T(8,128)(2,1)S(1)}, u32[]{:S(2)}, u32[]{:S(2)}) %collective-permute-start.16) | collective-permute-done | bytes 655392 | tf_op jit(solution)/shard_map/ppermute | solution.py:250
  89.6 1.0 %add_convert_fusion = bf16[64,5120]{1,0:T(8,128)(2,1)} fusion(f32[64,5120]{1,0:T(8,128)S(1)} %shard_map.113, bf16[64,5120]{1,0:T(8,128)(2,1)S(1)} %collective-permute-done.16), kind=kLoop, calls=%fused_computation | loop fusion | flops 983040 | bytes 2621440 | tf_op jit(solution)/shard_map/convert_element_type | solution.py:326
  (42 shorter events, 4.6 us)
Async XLA Ops:
  0.6 61.2 %collective-permute-start.8 = (bf16[384,5120]{1,0:T(8,128)(2,1)}, bf16[384,5120]{1,0:T(8,128)(2,1)}, u32[]{:S(2)}, u32[]{:S(2)}) collective-permute-start(bf16[384,5120]{1,0:T(8,128)(2,1)} %wa_ref.5), channel_id=1, source_target_pairs={{0,1},{1,0},{2,3},{3,2},{4,5},{5,4},{6,7},{7,6},{8,9},{9,8},{10,11... | collective-permute-start | bytes 11796488 | tf_op jit(solution)/shard_map/ppermute | solution.py:250
  3.9 12.0 %collective-permute-start = (bf16[64,5120]{1,0:T(8,128)(2,1)}, bf16[64,5120]{1,0:T(8,128)(2,1)S(1)}, u32[]{:S(2)}, u32[]{:S(2)}) collective-permute-start(bf16[64,5120]{1,0:T(8,128)(2,1)} %x1.1), channel_id=1, source_target_pairs={{0,2},{1,7},{2,4},{3,1},{4,6},{5,3},{6,0},{7,5},{8,10},{9,15},{10,... | collective-permute-start | bytes 1966088 | tf_op jit(solution)/shard_map/ppermute | solution.py:250
  4.7 12.8 %collective-permute-start.2 = (bf16[64,5120]{1,0:T(8,128)(2,1)}, bf16[64,5120]{1,0:T(8,128)(2,1)S(1)}, u32[]{:S(2)}, u32[]{:S(2)}) collective-permute-start(bf16[64,5120]{1,0:T(8,128)(2,1)} %x1.1), channel_id=1, source_target_pairs={{0,1},{1,0},{2,3},{3,2},{4,5},{5,4},{6,7},{7,6},{8,9},{9,8},{10,11... | collective-permute-start | bytes 1966088 | tf_op jit(solution)/shard_map/ppermute | solution.py:250
  4.7 25.4 %all-to-all-start = ((bf16[32,32,256]{2,1,0:T(8,128)(2,1)}), bf16[32,32,256]{2,1,0:T(8,128)(2,1)S(1)}, u32[]{:S(2)}, u32[]{:S(2)}) async-start(bf16[32,32,256]{2,1,0:T(8,128)(2,1)} %bitcast.4), calls=%async_computation | async-start | bytes 1048576 | tf_op jit(solution)/shard_map/all_to_all | solution.py:262
  15.9 4.2 %copy-start = (bf16[64,5120]{1,0:T(8,128)(2,1)S(1)}, bf16[64,5120]{1,0:T(8,128)(2,1)}, u32[]{:S(2)}) copy-start(bf16[64,5120]{1,0:T(8,128)(2,1)} %x1.1) | copy-start | bytes 1966084
  15.9 4.2 %copy-start.2 = (f32[5120]{0:T(1024)S(1)}, f32[5120]{0:T(1024)}, u32[]{:S(2)}) copy-start(f32[5120]{0:T(1024)} %param.9) | copy-start | bytes 61444
  15.9 4.2 %collective-permute-start.1 = (bf16[64,5120]{1,0:T(8,128)(2,1)S(1)}, bf16[64,5120]{1,0:T(8,128)(2,1)S(1)}, u32[]{:S(2)}, u32[]{:S(2)}) collective-permute-start(bf16[64,5120]{1,0:T(8,128)(2,1)S(1)} %collective-permute-done.x0), channel_id=1, source_target_pairs={{0,1},{1,0},{2,3},{3,2},{4,5},{5,4},{6,7},{7,6},{8,9},{9,8},{10,11... | collective-permute-start | bytes 1966088 | tf_op jit(solution)/shard_map/ppermute | solution.py:250
  16.8 22.4 %collective-permute-start.3 = (bf16[64,5120]{1,0:T(8,128)(2,1)S(1)}, bf16[64,5120]{1,0:T(8,128)(2,1)S(1)}, u32[]{:S(2)}, u32[]{:S(2)}) collective-permute-start(bf16[64,5120]{1,0:T(8,128)(2,1)S(1)} %collective-permute-done.x0), channel_id=1, source_target_pairs={{0,2},{1,7},{2,4},{3,1},{4,6},{5,3},{6,0},{7,5},{8,10},{9,15},{10,... | collective-permute-start | bytes 1966088 | tf_op jit(solution)/shard_map/ppermute | solution.py:250
  17.5 23.7 %collective-permute-start.4 = (bf16[64,5120]{1,0:T(8,128)(2,1)S(1)}, bf16[64,5120]{1,0:T(8,128)(2,1)}, u32[]{:S(2)}, u32[]{:S(2)}) collective-permute-start(bf16[64,5120]{1,0:T(8,128)(2,1)S(1)} %collective-permute-done.2.x3), channel_id=1, source_target_pairs={{0,2},{1,7},{2,4},{3,1},{4,6},{5,3},{6,0},{7,5},{8,10},{9,15},{10,... | collective-permute-start | bytes 1966088 | tf_op jit(solution)/shard_map/ppermute | solution.py:250
  20.1 4.5 %copy-start.4 = (bf16[2048,256]{1,0:T(8,128)(2,1)S(1)}, bf16[2048,256]{1,0:T(8,128)(2,1)}, u32[]{:S(2)}) copy-start(bf16[2048,256]{1,0:T(8,128)(2,1)} %prompt_ref.3) | copy-start | bytes 3145732
  24.6 5.5 %copy-start.3 = (s32[2,32]{1,0:T(2,128)S(1)}, s32[2,32]{1,0:T(2,128)}, u32[]{:S(2)}) copy-start(s32[2,32]{1,0:T(2,128)} %parents_ref.3) | copy-start | bytes 772
  27.2 0.7 copy-start.6
  31.6 22.7 %all-to-all-start.1 = ((bf16[32,72,128]{2,1,0:T(8,128)(2,1)}), bf16[32,72,128]{2,1,0:T(8,128)(2,1)S(1)}, u32[]{:S(2)}, u32[]{:S(2)}) async-start(bf16[32,72,128]{2,1,0:T(8,128)(2,1)} %shard_map.105), calls=%async_computation.1 | async-start | bytes 1179648 | tf_op jit(solution)/shard_map/all_to_all | solution.py:287
  39.2 10.1 %copy-start.5 = (bf16[2048,256]{1,0:T(8,128)(2,1)S(1)}, bf16[2048,256]{1,0:T(8,128)(2,1)}, u32[]{:S(2)}) copy-start(bf16[2048,256]{1,0:T(8,128)(2,1)} %prompt_ref.3) | copy-start | bytes 3145732
  39.2 10.1 %copy-start.7 = (f32[128,768]{1,0:T(8,128)S(1)}, f32[128,768]{1,0:T(8,128)}, u32[]{:S(2)}) copy-start(f32[128,768]{1,0:T(8,128)} %copy-done.6) | copy-start | bytes 1179652
  39.2 3.7 %collective-permute-start.5 = (bf16[64,5120]{1,0:T(8,128)(2,1)S(1)}, bf16[64,5120]{1,0:T(8,128)(2,1)S(1)}, u32[]{:S(2)}, u32[]{:S(2)}) collective-permute-start(bf16[64,5120]{1,0:T(8,128)(2,1)S(1)} %collective-permute-done.3.x0), channel_id=1, source_target_pairs={{0,1},{1,0},{2,3},{3,2},{4,5},{5,4},{6,7},{7,6},{8,9},{9,8},{10,11... | collective-permute-start | bytes 1966088 | tf_op jit(solution)/shard_map/ppermute | solution.py:250
  41.1 2.7 %collective-permute-start.6 = (bf16[64,5120]{1,0:T(8,128)(2,1)}, bf16[64,5120]{1,0:T(8,128)(2,1)S(1)}, u32[]{:S(2)}, u32[]{:S(2)}) collective-permute-start(bf16[64,5120]{1,0:T(8,128)(2,1)} %collective-permute-done.4.x1), channel_id=1, source_target_pairs={{0,1},{1,0},{2,3},{3,2},{4,5},{5,4},{6,7},{7,6},{8,9},{9,8},{10,11... | collective-permute-start | bytes 1966088 | tf_op jit(solution)/shard_map/ppermute | solution.py:250
  56.0 5.8 %collective-permute-start.9 = (bf16[128,384]{1,0:T(8,128)(2,1)S(1)}, bf16[128,384]{1,0:T(8,128)(2,1)S(1)}, u32[]{:S(2)}, u32[]{:S(2)}) collective-permute-start(bf16[128,384]{1,0:T(8,128)(2,1)S(1)} %get-tuple-element.45), channel_id=1, source_target_pairs={{0,1},{1,0},{2,3},{3,2},{4,5},{5,4},{6,7},{7,6},{8,9},{9,8},{10,11... | collective-permute-start | bytes 294920 | tf_op jit(solution)/shard_map/ppermute | solution.py:250
  64.5 13.6 %collective-permute-start.15 = (bf16[64,2560]{1,0:T(8,128)(2,1)S(1)}, bf16[64,2560]{1,0:T(8,128)(2,1)S(1)}, u32[]{:S(2)}, u32[]{:S(2)}) collective-permute-start(bf16[64,2560]{1,0:T(8,128)(2,1)S(1)} %get-tuple-element.50), channel_id=1, source_target_pairs={{2,0},{7,1},{4,2},{1,3},{6,4},{3,5},{0,6},{5,7},{10,8},{15,9},{12,... | collective-permute-start | bytes 983048 | tf_op jit(solution)/shard_map/ppermute | solution.py:250
  67.3 10.8 %collective-permute-start.14 = (bf16[64,2560]{1,0:T(8,128)(2,1)S(1)}, bf16[64,2560]{1,0:T(8,128)(2,1)S(1)}, u32[]{:S(2)}, u32[]{:S(2)}) collective-permute-start(bf16[64,2560]{1,0:T(8,128)(2,1)S(1)} %get-tuple-element.49), channel_id=1, source_target_pairs={{2,0},{7,1},{4,2},{1,3},{6,4},{3,5},{0,6},{5,7},{10,8},{15,9},{12,... | collective-permute-start | bytes 983048 | tf_op jit(solution)/shard_map/ppermute | solution.py:250
  70.3 2.9 %collective-permute-start.7 = (bf16[128,384]{1,0:T(8,128)(2,1)S(1)}, bf16[128,384]{1,0:T(8,128)(2,1)S(1)}, u32[]{:S(2)}, u32[]{:S(2)}) collective-permute-start(bf16[128,384]{1,0:T(8,128)(2,1)S(1)} %get-tuple-element.39), channel_id=1, source_target_pairs={{0,1},{1,0},{2,3},{3,2},{4,5},{5,4},{6,7},{7,6},{8,9},{9,8},{10,11... | collective-permute-start | bytes 294920 | tf_op jit(solution)/shard_map/ppermute | solution.py:250
  71.9 7.1 %collective-permute-start.12 = (bf16[64,2560]{1,0:T(8,128)(2,1)S(1)}, bf16[64,2560]{1,0:T(8,128)(2,1)S(1)}, u32[]{:S(2)}, u32[]{:S(2)}) collective-permute-start(bf16[64,2560]{1,0:T(8,128)(2,1)S(1)} %get-tuple-element.47), channel_id=1, source_target_pairs={{2,0},{7,1},{4,2},{1,3},{6,4},{3,5},{0,6},{5,7},{10,8},{15,9},{12,... | collective-permute-start | bytes 983048 | tf_op jit(solution)/shard_map/ppermute | solution.py:250
  72.3 10.4 %collective-permute-start.10 = (bf16[64,2560]{1,0:T(8,128)(2,1)S(1)}, bf16[64,2560]{1,0:T(8,128)(2,1)}, u32[]{:S(2)}, u32[]{:S(2)}) collective-permute-start(bf16[64,2560]{1,0:T(8,128)(2,1)S(1)} %get-tuple-element.46), channel_id=1, source_target_pairs={{2,0},{7,1},{4,2},{1,3},{6,4},{3,5},{0,6},{5,7},{10,8},{15,9},{12,... | collective-permute-start | bytes 983048 | tf_op jit(solution)/shard_map/ppermute | solution.py:250
  78.1 6.7 %copy-start.1 = (bf16[64,5120]{1,0:T(8,128)(2,1)S(1)}, bf16[64,5120]{1,0:T(8,128)(2,1)}, u32[]{:S(2)}) copy-start(bf16[64,5120]{1,0:T(8,128)(2,1)} %get-tuple-element.40.block_ref) | copy-start | bytes 1966084
  78.3 11.3 %collective-permute-start.16 = (bf16[64,5120]{1,0:T(8,128)(2,1)S(1)}, bf16[64,5120]{1,0:T(8,128)(2,1)S(1)}, u32[]{:S(2)}, u32[]{:S(2)}) collective-permute-start(bf16[64,5120]{1,0:T(8,128)(2,1)S(1)} %shard_map.114), channel_id=1, source_target_pairs={{2,0},{7,1},{4,2},{1,3},{6,4},{3,5},{0,6},{5,7},{10,8},{15,9},{12,... | collective-permute-start | bytes 1966088 | tf_op jit(solution)/shard_map/ppermute | solution.py:250
  79.1 5.7 %collective-permute-start.13 = (bf16[64,2560]{1,0:T(8,128)(2,1)S(1)}, bf16[64,2560]{1,0:T(8,128)(2,1)S(1)}, u32[]{:S(2)}, u32[]{:S(2)}) collective-permute-start(bf16[64,2560]{1,0:T(8,128)(2,1)S(1)} %collective-permute-done.12), channel_id=1, source_target_pairs={{0,1},{1,0},{2,3},{3,2},{4,5},{5,4},{6,7},{7,6},{8,9},{9,8},{10,11... | collective-permute-start | bytes 983048 | tf_op jit(solution)/shard_map/ppermute | solution.py:250
  82.7 2.1 %collective-permute-start.11 = (bf16[64,2560]{1,0:T(8,128)(2,1)}, bf16[64,2560]{1,0:T(8,128)(2,1)S(1)}, u32[]{:S(2)}, u32[]{:S(2)}) collective-permute-start(bf16[64,2560]{1,0:T(8,128)(2,1)} %collective-permute-done.10), channel_id=1, source_target_pairs={{0,1},{1,0},{2,3},{3,2},{4,5},{5,4},{6,7},{7,6},{8,9},{9,8},{10,11... | collective-permute-start | bytes 983048 | tf_op jit(solution)/shard_map/ppermute | solution.py:250
